TPU v7x, 128 devices: a whole 4x4x4 slice. The times are simulated.
128 devices in a mesh: batch: 32 (over z, y, x_hi), mp: 4 (over x_lo, core).
Axes of the slice: x: 4 (x_hi: 2, x_lo: 2; x = x_hi * 2 + x_lo), y: 4, z: 4, core: 2. Of those that a mesh axis runs over, the one named last changes fastest.
Arguments:
- lookup_ids: int32 [64, 65536], P('batch'), may hold values from 0 to 8191
- table_feature: int32 [64], replicated, may hold values from 0 to 63, each once
- tables: bfloat16 [64, 8192, 128], P('batch'), may hold values from -6 to 6
- cross_down: bfloat16 [2, 8192, 512], P(None, 'mp'), may hold values from -0.0625 to 0.0625
- cross_up: bfloat16 [2, 512, 8192], P(None, None, 'mp'), may hold values from -0.25 to 0.25
- cross_bias: float32 [2, 8192], P(None, 'mp'), may hold values from -3 to 3
Outputs:
- crossed: bfloat16 [65536, 8192], P('batch', 'mp')
Inputs may be any that keep to these rules, and one draw needn't show every extreme that they name: `table_feature`: each number appears once.
All inputs are finite; a program needn't handle non-finite values.
Results may differ from a plain program's by a relative error of at most 0.015.
Values may be sent and summed in bfloat16 or wider, within the bound.
No kernel may reach another device: no remote copies, remote signals or barrier semaphores. Data moves between devices by JAX's collectives and lax.ppermute only.
A program may use at most 128 MiB of HBM per device.

v0:
```python
import jax
import jax.numpy as jnp
from jax import lax
from jax.sharding import PartitionSpec as P


def in_blocks(x, dim, size):
    shape = x.shape
    parts = x.reshape(*shape[:dim], size, shape[dim] // size, *shape[dim + 1 :])
    return jnp.moveaxis(parts, dim, 0)


def laid_out(parts, dim):
    shape = list(parts.shape[1:])
    shape[dim] *= parts.shape[0]
    return jnp.moveaxis(parts, 0, dim).reshape(shape)


def one_exchange(x, axis, axes, splits, concats):
    sizes = [lax.axis_size(a) for a in axes]
    parts = in_blocks(x, splits[0], sizes[0])
    parts = jnp.moveaxis(in_blocks(parts, splits[1] + 1, sizes[1]), 0, 1)
    inside = parts.shape[2:]
    parts = parts.reshape(-1, *inside)
    parts = lax.all_to_all(parts, axis, split_axis=0, concat_axis=0, tiled=True)
    parts = laid_out(parts.reshape(*sizes, *inside), concats[0] + 1)
    return laid_out(parts, concats[1])


def sent_and_summed(x, axis, dim):
    size = lax.axis_size(axis)
    parts = lax.all_to_all(in_blocks(x, dim, size), axis, 0, 0, tiled=True)
    return jnp.sum(parts.astype(jnp.float32), axis=0)


def from_everyone(x, axis):
    size = lax.axis_size(axis)
    return lax.all_to_all(jnp.broadcast_to(x[None], (size, *x.shape)), axis, 0, 0, tiled=True)


def gathered_copies(x, axis, dim):
    return laid_out(from_everyone(x, axis), dim)


def per_device(lookup_ids, table_feature, tables, cross_down, cross_up, cross_bias):
    slots_local = tables.shape[0]
    feats = table_feature.shape[0]
    sources = lax.axis_size("batch")
    groups = lax.axis_size("mp")
    examples_local = lookup_ids.shape[1] // sources
    share = examples_local // groups
    start = lax.axis_index("mp") * share
    by_owner = lookup_ids.reshape(slots_local, sources, examples_local)
    wanted = lax.dynamic_slice_in_dim(by_owner, start, share, 2)
    looked = jnp.stack(
        [
            jnp.take(tables[slot], wanted[slot].reshape(sources * share), axis=0)
            for slot in range(slots_local)
        ],
        axis=1,
    )
    looked = looked.reshape(sources, share, slots_local, tables.shape[2])
    received = one_exchange(looked, ("batch", "mp"), ("batch", "mp"), (0, 3), (0, 1))
    emb_local = received.shape[3]
    unfolded = jnp.transpose(received, (1, 0, 2, 3)).reshape(examples_local, feats, emb_local)
    placing = (table_feature[:, None] == jnp.arange(feats, dtype=jnp.int32)[None, :]).astype(
        jnp.bfloat16
    )
    ordered = jnp.einsum("rse,sf->ref", unfolded, placing, preferred_element_type=jnp.float32)
    embedded = ordered.astype(jnp.bfloat16).reshape(examples_local, emb_local * feats)
    embedded_wide = embedded.astype(jnp.float32)
    state = embedded
    for layer in range(len(cross_down)):
        weight_down = cross_down[layer]
        current = state
        product = jnp.dot(current, weight_down, preferred_element_type=jnp.float32)
        mine = sent_and_summed(
            product.astype(jnp.bfloat16).astype(jnp.float32).astype(jnp.bfloat16), "mp", 0
        ).astype(jnp.bfloat16)
        low = gathered_copies(mine, "mp", 0)
        high = (
            jnp.dot(low, cross_up[layer], preferred_element_type=jnp.float32)
            + cross_bias[layer][None, :]
        )
        state = (embedded_wide * high + state.astype(jnp.float32)).astype(jnp.bfloat16)
    return state


def solution(mesh):
    return jax.shard_map(
        per_device,
        mesh=mesh,
        in_specs=(
            P("batch", None),
            P(),
            P("batch", None, None),
            P(None, "mp", None),
            P(None, None, "mp"),
            P(None, "mp"),
        ),
        out_specs=P("batch", "mp"),
        check_vma=False,
    )
```

profile of v0, /device:TPU:1, one launch (start us, length us, event | category | flops | bytes accessed | tf_op | source)
XLA Modules:
  0.0 462.9 jit_solution(5163655522445915869)
XLA Ops:
  0.0 1.3 copy.30
  1.5 3.8 slice_bitcast_fusion.1
  5.4 57.3 %gather_fusion = bf16[16384,128]{1,0:T(8,128)(2,1)} fusion(bf16[8192,128]{1,0:T(8,128)(2,1)} %get-tuple-element.6, s32[16384]{0:T(1024)S(1)} %fusion.16), kind=kCustom, calls=%fused_computation.clone | custom fusion | bytes 8454144 | tf_op jit(solution)/shard_map/jit(_take)/gather | solution.py:57
  62.7 11.5 %broadcast_select_fusion.1 = bf16[16384,128]{1,0:T(8,128)(2,1)} fusion(bf16[16384,128]{1,0:T(8,128)(2,1)} %gather_fusion, pred[16384]{0:T(1024)(128)(4,1)S(1)} %compare_and_fusion.1), kind=kLoop, calls=%fused_computation.12 | loop fusion | flops 2097152 | bytes 8404992 | tf_op jit(solution)/shard_map/jit(_take)/select_n | solution.py:57
  74.2 6.5 %copy.12 = bf16[16384,128]{0,1:T(8,128)(2,1)} copy(bf16[16384,128]{1,0:T(8,128)(2,1)} %broadcast_select_fusion.1) | data formatting | bytes 8388608 | tf_op jit(solution)/shard_map/jit(_take)/select_n | solution.py:57
  80.7 5.9 %copy.22 = bf16[16,8,32,512]{3,2,1,0:T(8,128)(2,1)} copy(bf16[16,8,32,512]{3,1,2,0:T(8,128)(2,1)} %bitcast.71) | data formatting | bytes 8388608
  86.5 57.9 %gather_fusion.1 = bf16[16384,128]{1,0:T(8,128)(2,1)} fusion(bf16[8192,128]{1,0:T(8,128)(2,1)S(1)} %get-tuple-element.7, s32[16384]{0:T(1024)S(1)} %fusion.17), kind=kCustom, calls=%fused_computation.1.clone | custom fusion | bytes 8454144 | tf_op jit(solution)/shard_map/jit(_take)/gather | solution.py:57
  144.4 11.5 %broadcast_select_fusion = bf16[16384,128]{1,0:T(8,128)(2,1)} fusion(bf16[16384,128]{1,0:T(8,128)(2,1)} %gather_fusion.1, pred[16384]{0:T(1024)(128)(4,1)S(1)} %compare_and_fusion), kind=kLoop, calls=%fused_computation.11 | loop fusion | flops 2097152 | bytes 8404992 | tf_op jit(solution)/shard_map/jit(_take)/select_n | solution.py:57
  155.9 6.5 %copy.13 = bf16[16384,128]{0,1:T(8,128)(2,1)} copy(bf16[16384,128]{1,0:T(8,128)(2,1)} %broadcast_select_fusion) | data formatting | bytes 8388608 | tf_op jit(solution)/shard_map/jit(_take)/select_n | solution.py:57
  162.4 0.0 copy-start.1
  162.4 6.0 %copy.24 = bf16[16,8,32,512]{3,2,1,0:T(8,128)(2,1)} copy(bf16[16,8,32,512]{3,1,2,0:T(8,128)(2,1)} %bitcast.72) | data formatting | bytes 8388608
  168.5 0.0 copy-done.1
  168.5 6.3 %maximum_bitcast_fusion = bf16[32,4,1,512,2,32]{3,0,5,1,4,2:T(8,128)(2,1)} fusion(bf16[32,1,512,1,4,32]{2,0,5,4,3,1:T(8,128)(2,1)} %bitcast.74, bf16[32,1,512,1,4,32]{2,0,5,4,3,1:T(8,128)(2,1)S(1)} %bitcast.73), kind=kLoop, calls=%fused_computation.7 | loop fusion | flops 4194304 | bytes 16777216 | tf_op jit(solution)/shard_map/transpose;transpose | solution.py:22
  174.8 11.3 %copy.14 = bf16[32,4,1,512,2,32]{3,5,4,2,1,0:T(8,128)(2,1)} copy(bf16[32,4,1,512,2,32]{3,0,5,1,4,2:T(8,128)(2,1)} %maximum_bitcast_fusion) | data formatting | bytes 16777216 | tf_op jit(solution)/shard_map/transpose;transpose | solution.py:22
  186.2 109.5 %all_to_all.25 = bf16[128,1,512,2,32]{2,4,3,1,0:T(8,128)(2,1)} all-to-all(bf16[128,1,512,2,32]{2,4,3,1,0:T(8,128)(2,1)} %bitcast.69), channel_id=1, replica_groups=mesh['batch'=32,'mp'=4] {'batch','mp'}, dimensions={0} | all-to-all | bytes 16777216 | tf_op jit(solution)/shard_map/all_to_all | solution.py:25
  295.6 0.0 copy-start.3
  295.6 8.1 %copy.19 = bf16[32,4,2,4,8,512]{5,4,1,3,2,0:T(8,128)(2,1)} copy(bf16[32,4,2,4,8,512]{5,4,3,2,1,0:T(8,128)(2,1)} %bitcast.70) | data formatting | bytes 16777216 | tf_op jit(solution)/shard_map/reshape | solution.py:16
  303.7 0.0 copy-done.3
  303.7 10.1 %fusion.5 = bf16[2048,32,64]{0,2,1:T(8,128)(2,1)S(1)} fusion(bf16[2048,64,32]{0,2,1:T(8,128)(2,1)} %bitcast.68, s32[64]{0:T(128)S(1)} %copy-done.3), kind=kOutput, calls=%fused_computation.10 | convolution fusion | flops 541069312 | bytes 16777472 | tf_op jit(solution)/shard_map/rse,sf->ref/dot_general | solution.py:69
  313.8 0.0 copy-start
  313.8 7.9 %convolution_convert_fusion.1 = bf16[2048,512]{1,0:T(8,128)(2,1)S(1)} fusion(bf16[2048,2048]{0,1:T(8,128)(2,1)S(1)} %bitcast.66, bf16[2,2048,512]{2,1,0:T(8,128)(2,1)} %param.11), kind=kOutput, calls=%fused_computation.14 | convolution fusion | flops 4296015872 | bytes 12582912 | tf_op jit(solution)/shard_map/dot_general | solution.py:76
  321.8 0.0 copy-done
  321.8 28.1 %all_to_all.26 = bf16[4,512,512]{2,1,0:T(8,128)(2,1)S(1)} all-to-all(bf16[4,512,512]{2,1,0:T(8,128)(2,1)S(1)} %bitcast.77), channel_id=1, replica_groups=mesh['batch'=32,'mp'=4] {'mp'}, dimensions={0} | all-to-all | bytes 4194304 | tf_op jit(solution)/shard_map/all_to_all | solution.py:32
  349.8 0.0 copy-start.2
  349.8 0.6 reduce_sum.24
  350.5 1.5 broadcast_in_dim.13
  352.0 4.6 all-to-all-start.2
  356.6 0.0 copy-done.2
  356.7 12.4 %copy.17 = bf16[2048,2048]{1,0:T(8,128)(2,1)} copy(bf16[2048,2048]{0,1:T(8,128)(2,1)} %bitcast.67) | data formatting | bytes 16777216 | tf_op jit(solution)/shard_map/reshape | solution.py:70
  369.0 12.3 %all-to-all-done.2 = bf16[4,512,512]{2,1,0:T(8,128)(2,1)S(1)} async-done(((bf16[4,512,512]{2,1,0:T(8,128)(2,1)}), bf16[4,512,512]{2,1,0:T(8,128)(2,1)S(1)}, u32[]{:S(2)}, u32[]{:S(2)}) %all-to-all-start.2) | async-done | bytes 2097184 | tf_op jit(solution)/shard_map/all_to_all | solution.py:38
  381.3 0.0 copy-start.4
  381.3 8.1 %fusion.2 = bf16[2048,2048]{1,0:T(8,128)(2,1)S(1)} fusion(bf16[2048,2048]{1,0:T(8,128)(2,1)} %copy.17, f32[2048]{0:T(1024)S(1)} %bitcast.86, bf16[2048,512]{1,0:T(8,128)(2,1)S(1)} %bitcast.75, bf16[2,512,2048]{2,1,0:T(8,128)(2,1)} %param.12), kind=kOutput, calls=%fused_computation.6 | convolution fusion | flops 4315938816 | bytes 20979712 | tf_op jit(solution)/shard_map/dot_general | solution.py:82
  389.4 0.0 copy-done.4
  389.4 0.0 copy-start.6
  389.4 4.9 %convolution_convert_fusion = bf16[2048,512]{1,0:T(8,128)(2,1)S(1)} fusion(bf16[2048,2048]{1,0:T(8,128)(2,1)S(1)} %fusion.2, bf16[2,2048,512]{2,1,0:T(8,128)(2,1)S(1)} %copy-done.4), kind=kOutput, calls=%fused_computation.13 | convolution fusion | flops 4296015872 | bytes 12582912 | tf_op jit(solution)/shard_map/dot_general | solution.py:76
  394.4 0.0 copy-done.6
  394.4 28.1 %all_to_all.27 = bf16[4,512,512]{2,1,0:T(8,128)(2,1)S(1)} all-to-all(bf16[4,512,512]{2,1,0:T(8,128)(2,1)S(1)} %bitcast.78), channel_id=1, replica_groups=mesh['batch'=32,'mp'=4] {'mp'}, dimensions={0} | all-to-all | bytes 4194304 | tf_op jit(solution)/shard_map/all_to_all | solution.py:32
  422.5 0.6 reduce_sum.25
  423.1 0.0 copy-start.5
  423.1 0.2 broadcast_in_dim.14
  423.3 28.4 %all_to_all.28 = bf16[4,512,512]{2,1,0:T(8,128)(2,1)S(1)} all-to-all(bf16[4,512,512]{2,1,0:T(8,128)(2,1)S(1)} %broadcast_in_dim.14), channel_id=1, replica_groups=mesh['batch'=32,'mp'=4] {'mp'}, dimensions={0} | all-to-all | bytes 4194304 | tf_op jit(solution)/shard_map/all_to_all | solution.py:38
  451.7 0.0 copy-done.5
  451.7 11.2 %fusion.1 = bf16[2048,2048]{1,0:T(8,128)(2,1)} fusion(bf16[2048,2048]{1,0:T(8,128)(2,1)} %copy.17, bf16[2048,2048]{1,0:T(8,128)(2,1)} %copy-done.6, f32[2048]{0:T(1024)S(1)} %bitcast.85, bf16[2048,512]{1,0:T(8,128)(2,1)S(1)} %bitcast.76, bf16[2,512,2048]{2,1,0:T(8,128)(2,1)S(1)} %copy-done.5), kind=kOutput, calls=%fused_computation.5 | convolution fusion | flops 4320133120 | bytes 29368320 | tf_op jit(solution)/shard_map/dot_general | solution.py:82
  (8 shorter events, 0.2 us)
Async XLA Ops:
  162.4 6.1 %copy-start.1 = (bf16[16,8,32,512]{3,2,1,0:T(8,128)(2,1)S(1)}, bf16[16,8,32,512]{3,2,1,0:T(8,128)(2,1)}, u32[]{:S(2)}) copy-start(bf16[16,8,32,512]{3,2,1,0:T(8,128)(2,1)} %copy.22) | copy-start | bytes 12582916
  295.6 8.1 %copy-start.3 = (s32[64]{0:T(128)S(1)}, s32[64]{0:T(128)}, u32[]{:S(2)}) copy-start(s32[64]{0:T(128)} %param.9) | copy-start | bytes 772
  313.8 8.0 %copy-start = (bf16[2048,32,64]{0,2,1:T(8,128)(2,1)}, bf16[2048,32,64]{0,2,1:T(8,128)(2,1)S(1)}, u32[]{:S(2)}) copy-start(bf16[2048,32,64]{0,2,1:T(8,128)(2,1)S(1)} %fusion.5) | copy-start | bytes 25165828
  349.8 6.8 %copy-start.2 = (f32[2,2048]{1,0:T(2,128)S(1)}, f32[2,2048]{1,0:T(2,128)}, u32[]{:S(2)}) copy-start(f32[2,2048]{1,0:T(2,128)} %param.13) | copy-start | bytes 49156
  352.0 29.3 %all-to-all-start.2 = ((bf16[4,512,512]{2,1,0:T(8,128)(2,1)}), bf16[4,512,512]{2,1,0:T(8,128)(2,1)S(1)}, u32[]{:S(2)}, u32[]{:S(2)}) async-start(bf16[4,512,512]{2,1,0:T(8,128)(2,1)} %broadcast_in_dim.13), calls=%async_computation.2 | async-start | bytes 4194304 | tf_op jit(solution)/shard_map/all_to_all | solution.py:38
  381.3 8.1 %copy-start.4 = (bf16[2,2048,512]{2,1,0:T(8,128)(2,1)S(1)}, bf16[2,2048,512]{2,1,0:T(8,128)(2,1)}, u32[]{:S(2)}) copy-start(bf16[2,2048,512]{2,1,0:T(8,128)(2,1)} %param.11) | copy-start | bytes 12582916
  389.4 5.0 %copy-start.6 = (bf16[2048,2048]{1,0:T(8,128)(2,1)}, bf16[2048,2048]{1,0:T(8,128)(2,1)S(1)}, u32[]{:S(2)}) copy-start(bf16[2048,2048]{1,0:T(8,128)(2,1)S(1)} %fusion.2) | copy-start | bytes 25165828
  423.1 28.6 %copy-start.5 = (bf16[2,512,2048]{2,1,0:T(8,128)(2,1)S(1)}, bf16[2,512,2048]{2,1,0:T(8,128)(2,1)}, u32[]{:S(2)}) copy-start(bf16[2,512,2048]{2,1,0:T(8,128)(2,1)} %param.12) | copy-start | bytes 12582916
where the time goes:
time: 465 us; the launch traced here: 463 us
  blocking collectives  194 us (42%)
  local copies, waits for them, and re-layouts  179 us (38%)
  matrix products  42.3 us (9%)
  other arithmetic  30.7 us (7%)
  waiting for transfers between devices  12.3 us (3%)
    gather x2, local copies, waits for them, and re-layouts, per_device(): jnp.take(tables[slot], wanted[slot].reshape(sources * share), axis=0)  115 us
    all_to_all x1, blocking collectives, one_exchange(): parts = lax.all_to_all(parts, axis, split_axis=0, concat_axis=0, tiled=True)  109 us
    all_to_all x2, blocking collectives, sent_and_summed(): parts = lax.all_to_all(in_blocks(x, dim, size), axis, 0, 0, tiled=True)  56.1 us
    all_to_all x1, blocking collectives, from_everyone(): lax.all_to_all(jnp.broadcast_to(x[None], (size, *x.shape)), axis, 0, 0, t...  28.4 us
    select_n x2, other arithmetic, per_device(): jnp.take(tables[slot], wanted[slot].reshape(sources * share), axis=0)  23 us
    dot_general x2, matrix products, per_device(): jnp.dot(low, cross_up[layer], preferred_element_type=jnp.float32)  19.3 us
    unnamed x20, local copies, waits for them, and re-layouts  13.4 us
    select_n x2, local copies, waits for them, and re-layouts, per_device(): jnp.take(tables[slot], wanted[slot].reshape(sources * share), axis=0)  13 us
  transfers between devices with their start and end apart: 1, of which 1 were waited for; matrix products, arithmetic and copies ran while one was open for 3% of the time, Pallas kernels for 0%

commit v1 on v0

v1 whole, which is shorter than its diff:
```python
import functools

import jax
import jax.numpy as jnp
from jax import lax
from jax.experimental import pallas as pl
from jax.experimental.pallas import tpu as pltpu
from jax.sharding import PartitionSpec as P

CHUNKS = 2
LANES = 128


def cost(flops, moved):
    return pl.CostEstimate(flops=flops, bytes_accessed=moved, transcendentals=0)


def gather_kernel(place, ids, tables, out, wide, even, odd):
    slots, rows, emb = tables.shape
    share = ids.shape[1]

    @pl.when(pl.program_id(0) == 0)
    def _():
        for slot in range(slots):
            wide[pl.ds(slot * rows, rows), :] = tables[slot].astype(jnp.float32)

    count = share // LANES
    for slot in range(slots):
        for group in range(count):
            held = even if (slot * count + group) % 2 == 0 else odd
            for row in range(LANES):
                index = ids[slot, group * LANES + row] + slot * rows
                held[pl.ds(row, 1), :] = wide[pl.ds(index, 1), :]
            turned = held[...].T.astype(jnp.bfloat16)
            out[0, :, slot, :, group * LANES : (group + 1) * LANES] = turned.reshape(
                out.shape[1], out.shape[3], LANES
            )


def looked_up(ids, tables, place, chunk, sources, groups, share):
    slots, rows, emb = tables.shape
    part = share // CHUNKS
    return pl.pallas_call(
        gather_kernel,
        grid_spec=pltpu.PrefetchScalarGridSpec(
            num_scalar_prefetch=1,
            grid=(sources,),
            in_specs=[
                pl.BlockSpec(
                    (slots, part),
                    lambda i, place: (0, (i * groups + place[0]) * CHUNKS + chunk),
                    memory_space=pltpu.SMEM,
                ),
                pl.BlockSpec((slots, rows, emb), lambda i, place: (0, 0, 0)),
            ],
            out_specs=pl.BlockSpec(
                (1, groups, slots, emb // groups, part), lambda i, place: (i, 0, 0, 0, 0)
            ),
            scratch_shapes=[
                pltpu.VMEM((slots * rows, emb), jnp.float32),
                pltpu.VMEM((LANES, emb), jnp.float32),
                pltpu.VMEM((LANES, emb), jnp.float32),
            ],
        ),
        out_shape=jax.ShapeDtypeStruct(
            (sources, groups, slots, emb // groups, part), jnp.bfloat16
        ),
        cost_estimate=cost(30_000_000_000 // CHUNKS, 12_000_000 // CHUNKS),
        name="lookup",
    )(place, ids, tables)


def first_kernel(order, moved, down, embedded, product, wide):
    feats, emb = order.shape[0], moved.shape[3]
    for feat in range(feats):
        slot = order[feat]
        wide[feat * emb : (feat + 1) * emb, :] = moved[slot // 2, 0, slot % 2].astype(jnp.float32)
    for pair in range(emb // 2):
        block = jnp.concatenate(
            [wide[pl.ds(2 * pair + k, feats, stride=emb), :] for k in range(2)], axis=0
        )
        embedded[:, pair * 2 * feats : (pair + 1) * 2 * feats] = block.T.astype(jnp.bfloat16)
    product[...] = jnp.dot(
        embedded[...], down[0], preferred_element_type=jnp.float32
    ).astype(jnp.bfloat16)


def first(moved, order, down):
    sources, groups, slots, emb, part = moved.shape
    feats = order.shape[0]
    width = feats * emb
    rank = down.shape[2]
    blocks = part // LANES
    return pl.pallas_call(
        first_kernel,
        grid_spec=pltpu.PrefetchScalarGridSpec(
            num_scalar_prefetch=1,
            grid=(groups * blocks,),
            in_specs=[
                pl.BlockSpec(
                    (sources, 1, slots, emb, LANES),
                    lambda i, order: (0, i // blocks, 0, 0, i % blocks),
                ),
                pl.BlockSpec((1, width, rank), lambda i, order: (0, 0, 0)),
            ],
            out_specs=[
                pl.BlockSpec((LANES, width), lambda i, order: (i, 0)),
                pl.BlockSpec((LANES, rank), lambda i, order: (i, 0)),
            ],
            scratch_shapes=[pltpu.VMEM((width, LANES), jnp.float32)],
        ),
        out_shape=[
            jax.ShapeDtypeStruct((groups * part, width), jnp.bfloat16),
            jax.ShapeDtypeStruct((groups * part, rank), jnp.bfloat16),
        ],
        cost_estimate=cost(2 * groups * part * width * rank, 4 * groups * part * width),
        name="first",
    )(order, moved, down)


def middle_kernel(low, embedded, up, bias, down, state, product):
    high = jnp.dot(low[...], up[0], preferred_element_type=jnp.float32) + bias[0:1, :]
    own = embedded[...].astype(jnp.float32)
    state[...] = (own * high + own).astype(jnp.bfloat16)
    product[...] = jnp.dot(
        state[...], down[0], preferred_element_type=jnp.float32
    ).astype(jnp.bfloat16)


def middle(low, embedded, up, bias, down, layer):
    rows, width = embedded.shape
    rank = low.shape[1]
    tall = min(rows, 256)
    return pl.pallas_call(
        middle_kernel,
        grid=(rows // tall,),
        in_specs=[
            pl.BlockSpec((tall, rank), lambda i: (i, 0)),
            pl.BlockSpec((tall, width), lambda i: (i, 0)),
            pl.BlockSpec((1, rank, width), lambda i: (layer, 0, 0)),
            pl.BlockSpec((1, width), lambda i: (0, 0)),
            pl.BlockSpec((1, width, rank), lambda i: (layer + 1, 0, 0)),
        ],
        out_specs=[
            pl.BlockSpec((tall, width), lambda i: (i, 0)),
            pl.BlockSpec((tall, rank), lambda i: (i, 0)),
        ],
        out_shape=[
            jax.ShapeDtypeStruct((rows, width), jnp.bfloat16),
            jax.ShapeDtypeStruct((rows, rank), jnp.bfloat16),
        ],
        cost_estimate=cost(4 * rows * width * rank, 4 * rows * width),
        name="middle",
    )(low, embedded, up, bias[layer : layer + 1], down)


def last_kernel(low, embedded, state, up, bias, *rest):
    out = rest[-1]
    high = jnp.dot(low[...], up[0], preferred_element_type=jnp.float32) + bias[0:1, :]
    out[...] = (
        embedded[...].astype(jnp.float32) * high + state[...].astype(jnp.float32)
    ).astype(jnp.bfloat16)


def last(low, embedded, state, up, bias, layer, chunk, so_far, total):
    rows, width = embedded.shape
    rank = low.shape[1]
    groups = N_GROUPS
    tall = rows // groups
    in_specs = [
        pl.BlockSpec((tall, rank), lambda i: (i, 0)),
        pl.BlockSpec((tall, width), lambda i: (i, 0)),
        pl.BlockSpec((tall, width), lambda i: (i, 0)),
        pl.BlockSpec((1, rank, width), lambda i: (layer, 0, 0)),
        pl.BlockSpec((1, width), lambda i: (0, 0)),
    ]
    args = [low, embedded, state, up, bias[layer : layer + 1]]
    aliases = {}
    if so_far is not None:
        in_specs.append(pl.BlockSpec(memory_space=pl.ANY))
        args.append(so_far)
        aliases = {5: 0}
    return pl.pallas_call(
        last_kernel,
        grid=(groups,),
        in_specs=in_specs,
        out_specs=pl.BlockSpec((tall, width), lambda i: (i * CHUNKS + chunk, 0)),
        out_shape=jax.ShapeDtypeStruct((total, width), jnp.bfloat16),
        input_output_aliases=aliases,
        cost_estimate=cost(2 * rows * width * rank, 6 * rows * width),
        name="last",
    )(*args)


N_GROUPS = 4
CORE = [(0, 1), (1, 0), (2, 3), (3, 2)]
CHIP = [(0, 2), (2, 0), (1, 3), (3, 1)]


def added(a, b):
    return (a.astype(jnp.float32) + b.astype(jnp.float32)).astype(jnp.bfloat16)


def summed(x):
    core = lax.axis_index("mp") % 2
    half = x.shape[0] // 2
    mine = lax.dynamic_slice_in_dim(x, core * half, half, 0)
    other = lax.dynamic_slice_in_dim(x, (1 - core) * half, half, 0)
    pair = added(mine, lax.ppermute(other, "mp", CORE))
    whole = added(pair, lax.ppermute(pair, "mp", CHIP))
    rest = lax.ppermute(whole, "mp", CORE)
    return jnp.concatenate(
        [jnp.where(core == 0, whole, rest), jnp.where(core == 0, rest, whole)], axis=0
    )


def per_device(lookup_ids, table_feature, tables, cross_down, cross_up, cross_bias):
    feats = table_feature.shape[0]
    sources = lax.axis_size("batch")
    groups = lax.axis_size("mp")
    total = lookup_ids.shape[1] // sources
    share = total // groups
    place = lax.axis_index("mp").reshape(1).astype(jnp.int32)
    slots = jnp.arange(feats, dtype=jnp.int32)
    order = jnp.sum(
        jnp.where(table_feature[None, :] == slots[:, None], slots[None, :], 0), axis=1
    ).astype(jnp.int32)
    out = None
    for chunk in range(CHUNKS):
        looked = looked_up(lookup_ids, tables, place, chunk, sources, groups, share)
        shape = looked.shape
        moved = lax.all_to_all(
            looked.reshape(sources * groups, *shape[2:]), ("batch", "mp"), 0, 0, tiled=True
        ).reshape(shape)
        embedded, product = first(moved, order, cross_down)
        state, product = middle(summed(product), embedded, cross_up, cross_bias, cross_down, 0)
        out = last(
            summed(product), embedded, state, cross_up, cross_bias, 1, chunk, out, total
        )
    return out


def solution(mesh):
    return jax.shard_map(
        per_device,
        mesh=mesh,
        in_specs=(
            P("batch", None),
            P(),
            P("batch", None, None),
            P(None, "mp", None),
            P(None, None, "mp"),
            P(None, "mp"),
        ),
        out_specs=P("batch", "mp"),
        check_vma=False,
    )
```

time: 465 us -> 262 us (0.56)
  blocking collectives: 194 us -> 0 us
  local copies, waits for them, and re-layouts: 179 us -> 4.95 us
  Pallas kernels: 0 us -> 114 us
  waiting for transfers between devices: 12.3 us -> 105 us
  matrix products: 42.3 us -> 0 us
  starting transfers between devices: 4.61 us -> 27.3 us
  other arithmetic: 30.7 us -> 8.3 us
    all_to_all x4 -> x0, blocking collectives: 194 us -> none  [the longest x1 109 us: one_exchange(): parts = lax.all_to_all(parts, axis, split_axis=0, concat_axis=0, tiled=True)]
    gather x2 -> x0, local copies, waits for them, and re-layouts: 115 us -> none  [per_device(): jnp.take(tables[slot], wanted[slot].reshape(sources * share), axis=0)]
    pallas_call x0 -> x8, Pallas kernels: none -> 114 us  [the longest x2 48 us: looked_up(): pl.pallas_call(gather_kernel, grid_spec=pltpu.PrefetchScalarGridSpec(num_...]
    all_to_all x1 -> x2, waiting for transfers between devices: 12.3 us -> 62.6 us  [per_device(): lax.all_to_all(looked.reshape(sources * groups, *shape[2:]), ('batch', 'm...]
    dot_general x5 -> x0, matrix products: 42.3 us -> none  [the longest x2 19.3 us: per_device(): jnp.dot(low, cross_up[layer], preferred_element_type=jnp.float32)]
    ppermute x0 -> x12, waiting for transfers between devices: none -> 42.2 us  [the longest x4 39.8 us: summed(): whole = added(pair, lax.ppermute(pair, 'mp', CHIP))]
    select_n x2 -> x4, other arithmetic: 23 us -> 0.29 us  [summed(): jnp.where(core == 0, whole, rest)]
    reshape x2 -> x0, local copies, waits for them, and re-layouts: 20.5 us -> none  [the longest x1 12.4 us: per_device(): ordered.astype(jnp.bfloat16).reshape(examples_local, emb_local * feats)]
  transfers between devices with their start and end apart: 1 -> 14, of which waited for: 1 -> 9; matrix products, arithmetic and copies ran while one was open for 3% -> 5% of each run, Pallas kernels for 0% -> 28%
where the time goes in v1:
time: 262 us; the launch traced here: 259 us
  Pallas kernels  114 us (44%)
  waiting for transfers between devices  105 us (40%)
  starting transfers between devices  27.3 us (10%)
  other arithmetic  8.3 us (3%)
  local copies, waits for them, and re-layouts  4.95 us (2%)
    all_to_all x2, waiting for transfers between devices, per_device(): lax.all_to_all(looked.reshape(sources * groups, *shape[2:]), ('batch', 'm...  62.6 us
    pallas_call x2, Pallas kernels, looked_up(): pl.pallas_call(gather_kernel, grid_spec=pltpu.PrefetchScalarGridSpec(num_...  48 us
    ppermute x4, waiting for transfers between devices, summed(): whole = added(pair, lax.ppermute(pair, 'mp', CHIP))  39.8 us
    pallas_call x2, Pallas kernels, first(): pl.pallas_call(first_kernel, grid_spec=pltpu.PrefetchScalarGridSpec(num_s...  31 us
    pallas_call x2, Pallas kernels, middle(): pl.pallas_call(middle_kernel, grid=(rows // tall,), in_specs=[pl.BlockSpe...  17.8 us
    all_to_all x2, starting transfers between devices, per_device(): lax.all_to_all(looked.reshape(sources * groups, *shape[2:]), ('batch', 'm...  17.6 us
    pallas_call x2, Pallas kernels, last(): pl.pallas_call(last_kernel, grid=(groups,), in_specs=in_specs, out_specs=...  17 us
  transfers between devices with their start and end apart: 14, of which 9 were waited for; matrix products, arithmetic and copies ran while one was open for 5% of the time, Pallas kernels for 28%

profile of v1, /device:TPU:1, one launch (start us, length us, event | category | flops | bytes accessed | tf_op | source)
XLA Modules:
  0.0 259.5 jit_solution(15425504548187922821)
XLA Ops:
  0.0 24.0 %lookup.3 = bf16[32,4,2,32,256]{4,3,2,1,0:T(8,128)(2,1)} custom-call(s32[1]{0:T(128)} %bitcast.place, s32[2,65536]{1,0:T(2,128)} %ids.3, bf16[2,8192,128]{2,1,0:T(8,128)(2,1)} %tables.3), custom_call_target="tpu_custom_call" | custom-call | flops 15000000512 | bytes 6000000 | tf_op jit(solution)/shard_map/lookup/pallas_call | solution.py:43
  24.0 11.9 %all-to-all-start.1 = ((bf16[128,2,32,256]{3,2,1,0:T(8,128)(2,1)}), bf16[128,2,32,256]{3,2,1,0:T(8,128)(2,1)}, u32[]{:S(2)}, u32[]{:S(2)}) async-start(bf16[128,2,32,256]{3,2,1,0:T(8,128)(2,1)} %bitcast.6), calls=%async_computation.1 | async-start | bytes 8388608 | tf_op jit(solution)/shard_map/all_to_all | solution.py:232
  36.0 24.0 %lookup.2 = bf16[32,4,2,32,256]{4,3,2,1,0:T(8,128)(2,1)} custom-call(s32[1]{0:T(128)} %bitcast.place, s32[2,65536]{1,0:T(2,128)} %ids.3, bf16[2,8192,128]{2,1,0:T(8,128)(2,1)} %tables.3), custom_call_target="tpu_custom_call" | custom-call | flops 15000000512 | bytes 6000000 | tf_op jit(solution)/shard_map/lookup/pallas_call | solution.py:43
  60.0 28.5 %all-to-all-done.1 = bf16[128,2,32,256]{3,2,1,0:T(8,128)(2,1)} async-done(((bf16[128,2,32,256]{3,2,1,0:T(8,128)(2,1)}), bf16[128,2,32,256]{3,2,1,0:T(8,128)(2,1)}, u32[]{:S(2)}, u32[]{:S(2)}) %all-to-all-start.1) | async-done | bytes 4194336 | tf_op jit(solution)/shard_map/all_to_all | solution.py:232
  88.5 5.7 %all-to-all-start = ((bf16[128,2,32,256]{3,2,1,0:T(8,128)(2,1)}), bf16[128,2,32,256]{3,2,1,0:T(8,128)(2,1)}, u32[]{:S(2)}, u32[]{:S(2)}) async-start(bf16[128,2,32,256]{3,2,1,0:T(8,128)(2,1)} %bitcast.5), calls=%async_computation | async-start | bytes 8388608 | tf_op jit(solution)/shard_map/all_to_all | solution.py:232
  94.2 0.7 select_reduce_fusion.order
  94.9 15.5 %first.3 = (bf16[1024,2048]{1,0:T(8,128)(2,1)}, bf16[1024,512]{1,0:T(8,128)(2,1)}) custom-call(s32[64]{0:T(128)} %select_reduce_fusion.order, bf16[32,4,2,32,256]{4,3,2,1,0:T(8,128)(2,1)} %bitcast.4.moved, bf16[2,2048,512]{2,1,0:T(8,128)(2,1)} %down.7), custom_call_target="tpu_custom_call" | custom-call | flops 2147483648 | bytes 8388608 | tf_op jit(solution)/shard_map/first/pallas_call | solution.py:94
  110.4 1.1 constant_dynamic-slice_fusion
  111.5 1.4 collective-permute-start.6
  112.8 34.1 %all-to-all-done = bf16[128,2,32,256]{3,2,1,0:T(8,128)(2,1)} async-done(((bf16[128,2,32,256]{3,2,1,0:T(8,128)(2,1)}), bf16[128,2,32,256]{3,2,1,0:T(8,128)(2,1)}, u32[]{:S(2)}, u32[]{:S(2)}) %all-to-all-start) | async-done | bytes 4194336 | tf_op jit(solution)/shard_map/all_to_all | solution.py:232
  146.9 15.5 %first.2 = (bf16[1024,2048]{1,0:T(8,128)(2,1)}, bf16[1024,512]{1,0:T(8,128)(2,1)}) custom-call(s32[64]{0:T(128)} %select_reduce_fusion.order, bf16[32,4,2,32,256]{4,3,2,1,0:T(8,128)(2,1)} %bitcast.2.moved, bf16[2,2048,512]{2,1,0:T(8,128)(2,1)} %down.7), custom_call_target="tpu_custom_call" | custom-call | flops 2147483648 | bytes 8388608 | tf_op jit(solution)/shard_map/first/pallas_call | solution.py:94
  162.5 1.1 constant_dynamic-slice_fusion.2
  163.6 1.0 collective-permute-start
  164.6 0.1 add_convert_fusion.3
  164.7 0.4 collective-permute-start.7
  165.1 1.0 collective-permute-done
  166.1 1.2 add_convert_fusion.7
  167.3 0.4 collective-permute-start.1
  167.7 10.6 %collective-permute-done.7 = bf16[512,512]{1,0:T(8,128)(2,1)S(1)} collective-permute-done((bf16[512,512]{1,0:T(8,128)(2,1)S(1)}, bf16[512,512]{1,0:T(8,128)(2,1)S(1)}, u32[]{:S(2)}, u32[]{:S(2)}) %collective-permute-start.7) | collective-permute-done | bytes 524320 | tf_op jit(solution)/shard_map/ppermute | solution.py:210
  178.3 0.1 add_convert_fusion.2
  178.4 1.5 collective-permute-start.8
  179.9 0.6 fusion
  180.5 9.0 %collective-permute-done.1 = bf16[512,512]{1,0:T(8,128)(2,1)S(1)} collective-permute-done((bf16[512,512]{1,0:T(8,128)(2,1)S(1)}, bf16[512,512]{1,0:T(8,128)(2,1)S(1)}, u32[]{:S(2)}, u32[]{:S(2)}) %collective-permute-start.1) | collective-permute-done | bytes 524320 | tf_op jit(solution)/shard_map/ppermute | solution.py:210
  189.5 0.1 add_convert_fusion.6
  189.6 1.0 collective-permute-start.2
  190.7 1.0 pad_maximum_fusion.2.low
  191.7 8.9 %middle.3 = (bf16[1024,2048]{1,0:T(8,128)(2,1)}, bf16[1024,512]{1,0:T(8,128)(2,1)}) custom-call(bf16[1024,512]{1,0:T(8,128)(2,1)} %pad_maximum_fusion.2.low, bf16[1024,2048]{1,0:T(8,128)(2,1)} %get-tuple-element.18.embedded, bf16[2,512,2048]{2,1,0:T(8,128)(2,1)} %up.7, f32[1,2048]{1,0:T(1,128)} %get-tuple-element.30.bias, bf16[2,2048,512]{2,1,0:T(8,128)(2,1)} %down.7), custom_call_target="tpu_custom_call" | custom-call | flops 4294967296 | bytes 8388608 | tf_op jit(solution)/shard_map/middle/pallas_call | solution.py:134
  200.6 1.1 constant_dynamic-slice_fusion.3
  201.9 1.0 pad_maximum_fusion.low
  202.9 9.0 %middle.2 = (bf16[1024,2048]{1,0:T(8,128)(2,1)}, bf16[1024,512]{1,0:T(8,128)(2,1)}) custom-call(bf16[1024,512]{1,0:T(8,128)(2,1)} %pad_maximum_fusion.low, bf16[1024,2048]{1,0:T(8,128)(2,1)} %get-tuple-element.14.embedded, bf16[2,512,2048]{2,1,0:T(8,128)(2,1)} %up.7, f32[1,2048]{1,0:T(1,128)} %get-tuple-element.30.bias, bf16[2,2048,512]{2,1,0:T(8,128)(2,1)} %down.7), custom_call_target="tpu_custom_call" | custom-call | flops 4294967296 | bytes 8388608 | tf_op jit(solution)/shard_map/middle/pallas_call | solution.py:134
  211.9 1.1 constant_dynamic-slice_fusion.1
  213.0 0.8 collective-permute-start.3
  213.7 0.1 add_convert_fusion.1
  213.9 0.4 collective-permute-start.10
  214.3 1.0 collective-permute-done.3
  215.3 1.2 add_convert_fusion.5
  216.4 0.4 collective-permute-start.4
  216.8 10.6 %collective-permute-done.10 = bf16[512,512]{1,0:T(8,128)(2,1)S(1)} collective-permute-done((bf16[512,512]{1,0:T(8,128)(2,1)S(1)}, bf16[512,512]{1,0:T(8,128)(2,1)S(1)}, u32[]{:S(2)}, u32[]{:S(2)}) %collective-permute-start.10) | collective-permute-done | bytes 524320 | tf_op jit(solution)/shard_map/ppermute | solution.py:210
  227.4 0.1 add_convert_fusion
  227.5 1.5 collective-permute-start.11
  229.0 9.6 %collective-permute-done.4 = bf16[512,512]{1,0:T(8,128)(2,1)S(1)} collective-permute-done((bf16[512,512]{1,0:T(8,128)(2,1)S(1)}, bf16[512,512]{1,0:T(8,128)(2,1)S(1)}, u32[]{:S(2)}, u32[]{:S(2)}) %collective-permute-start.4) | collective-permute-done | bytes 524320 | tf_op jit(solution)/shard_map/ppermute | solution.py:210
  238.6 0.1 add_convert_fusion.4
  238.8 1.0 collective-permute-start.5
  239.8 1.0 pad_maximum_fusion.3.low
  240.9 0.4 collective-permute-done.5
  241.4 1.1 pad_maximum_fusion.1.low
  242.4 8.5 %last.2.rest_0_ = bf16[2048,2048]{1,0:T(8,128)(2,1)} custom-call(bf16[1024,512]{1,0:T(8,128)(2,1)} %pad_maximum_fusion.3.low, bf16[1024,2048]{1,0:T(8,128)(2,1)} %get-tuple-element.18.embedded, bf16[1024,2048]{1,0:T(8,128)(2,1)} %get-tuple-element.20.state, bf16[2,512,2048]{2,1,0:T(8,128)(2,1)} %up.7, f32[1,2048]{1,0:T(1,128)} %get-tuple-element.29.bias), custom_call_target="tpu_custom_call" | custom-call | flops 2147483648 | bytes 12582912 | tf_op jit(solution)/shard_map/last/pallas_call | solution.py:183
  250.9 8.5 %last.3 = bf16[2048,2048]{1,0:T(8,128)(2,1)} custom-call(bf16[1024,512]{1,0:T(8,128)(2,1)} %pad_maximum_fusion.1.low, bf16[1024,2048]{1,0:T(8,128)(2,1)} %get-tuple-element.14.embedded, bf16[1024,2048]{1,0:T(8,128)(2,1)} %get-tuple-element.16.state, bf16[2,512,2048]{2,1,0:T(8,128)(2,1)} %up.7, ...), custom_call_target="tpu_custom_call", output_to_operand_aliasing={{}: (5, {})} | custom-call | flops 2147483648 | bytes 12582912 | tf_op jit(solution)/shard_map/last/pallas_call | solution.py:183
  (18 shorter events, 0.4 us)
Async XLA Ops:
  24.0 64.5 %all-to-all-start.1 = ((bf16[128,2,32,256]{3,2,1,0:T(8,128)(2,1)}), bf16[128,2,32,256]{3,2,1,0:T(8,128)(2,1)}, u32[]{:S(2)}, u32[]{:S(2)}) async-start(bf16[128,2,32,256]{3,2,1,0:T(8,128)(2,1)} %bitcast.6), calls=%async_computation.1 | async-start | bytes 8388608 | tf_op jit(solution)/shard_map/all_to_all | solution.py:232
  88.5 5.7 %copy-start.3 = (s32[64]{0:T(128)S(1)}, s32[64]{0:T(128)}, u32[]{:S(2)}) copy-start(s32[64]{0:T(128)} %param.7) | copy-start | bytes 772
  88.5 58.4 %all-to-all-start = ((bf16[128,2,32,256]{3,2,1,0:T(8,128)(2,1)}), bf16[128,2,32,256]{3,2,1,0:T(8,128)(2,1)}, u32[]{:S(2)}, u32[]{:S(2)}) async-start(bf16[128,2,32,256]{3,2,1,0:T(8,128)(2,1)} %bitcast.5), calls=%async_computation | async-start | bytes 8388608 | tf_op jit(solution)/shard_map/all_to_all | solution.py:232
  111.5 53.1 %collective-permute-start.6 = (bf16[512,512]{1,0:T(8,128)(2,1)S(1)}, bf16[512,512]{1,0:T(8,128)(2,1)S(1)}, u32[]{:S(2)}, u32[]{:S(2)}) collective-permute-start(bf16[512,512]{1,0:T(8,128)(2,1)S(1)} %constant_dynamic-slice_fusion), channel_id=1, source_target_pairs={{0,1},{1,0},{2,3},{3,2},{4,5},{5,4},{6,7},{7,6},{8,9},{9,8},{10,11... | collective-permute-start | bytes 1572872 | tf_op jit(solution)/shard_map/ppermute | solution.py:209
  146.9 17.7 %copy-start = (bf16[1024,512]{1,0:T(8,128)(2,1)S(1)}, bf16[1024,512]{1,0:T(8,128)(2,1)}, u32[]{:S(2)}) copy-start(bf16[1024,512]{1,0:T(8,128)(2,1)} %get-tuple-element.17) | copy-start | bytes 3145732
  162.5 17.4 %copy-start.2 = (f32[2,2048]{1,0:T(2,128)S(1)}, f32[2,2048]{1,0:T(2,128)}, u32[]{:S(2)}) copy-start(f32[2,2048]{1,0:T(2,128)} %param.11) | copy-start | bytes 49156
  163.6 2.6 collective-permute-start
  164.7 13.5 %collective-permute-start.7 = (bf16[512,512]{1,0:T(8,128)(2,1)S(1)}, bf16[512,512]{1,0:T(8,128)(2,1)S(1)}, u32[]{:S(2)}, u32[]{:S(2)}) collective-permute-start(bf16[512,512]{1,0:T(8,128)(2,1)S(1)} %add_convert_fusion.3), channel_id=1, source_target_pairs={{0,2},{2,0},{1,3},{3,1},{4,6},{6,4},{5,7},{7,5},{8,10},{10,8},{9,1... | collective-permute-start | bytes 1572872 | tf_op jit(solution)/shard_map/ppermute | solution.py:210
  167.3 22.2 %collective-permute-start.1 = (bf16[512,512]{1,0:T(8,128)(2,1)S(1)}, bf16[512,512]{1,0:T(8,128)(2,1)S(1)}, u32[]{:S(2)}, u32[]{:S(2)}) collective-permute-start(bf16[512,512]{1,0:T(8,128)(2,1)S(1)} %add_convert_fusion.7), channel_id=1, source_target_pairs={{0,2},{2,0},{1,3},{3,1},{4,6},{6,4},{5,7},{7,5},{8,10},{10,8},{9,1... | collective-permute-start | bytes 1572872 | tf_op jit(solution)/shard_map/ppermute | solution.py:210
  178.4 12.2 %collective-permute-start.8 = (bf16[512,512]{1,0:T(8,128)(2,1)S(1)}, bf16[512,512]{1,0:T(8,128)(2,1)S(1)}, u32[]{:S(2)}, u32[]{:S(2)}) collective-permute-start(bf16[512,512]{1,0:T(8,128)(2,1)S(1)} %add_convert_fusion.2), channel_id=1, source_target_pairs={{0,1},{1,0},{2,3},{3,2},{4,5},{5,4},{6,7},{7,6},{8,9},{9,8},{10,11... | collective-permute-start | bytes 1572872 | tf_op jit(solution)/shard_map/ppermute | solution.py:211
  189.6 12.2 %collective-permute-start.2 = (bf16[512,512]{1,0:T(8,128)(2,1)S(1)}, bf16[512,512]{1,0:T(8,128)(2,1)S(1)}, u32[]{:S(2)}, u32[]{:S(2)}) collective-permute-start(bf16[512,512]{1,0:T(8,128)(2,1)S(1)} %add_convert_fusion.6), channel_id=1, source_target_pairs={{0,1},{1,0},{2,3},{3,2},{4,5},{5,4},{6,7},{7,6},{8,9},{9,8},{10,11... | collective-permute-start | bytes 1572872 | tf_op jit(solution)/shard_map/ppermute | solution.py:211
  201.7 12.0 %collective-permute-start.9 = (bf16[512,512]{1,0:T(8,128)(2,1)S(1)}, bf16[512,512]{1,0:T(8,128)(2,1)S(1)}, u32[]{:S(2)}, u32[]{:S(2)}) collective-permute-start(bf16[512,512]{1,0:T(8,128)(2,1)S(1)} %constant_dynamic-slice_fusion.3), channel_id=1, source_target_pairs={{0,1},{1,0},{2,3},{3,2},{4,5},{5,4},{6,7},{7,6},{8,9},{9,8},{10,11... | collective-permute-start | bytes 1572872 | tf_op jit(solution)/shard_map/ppermute | solution.py:209
  202.9 10.8 %copy-start.1 = (bf16[1024,512]{1,0:T(8,128)(2,1)S(1)}, bf16[1024,512]{1,0:T(8,128)(2,1)}, u32[]{:S(2)}) copy-start(bf16[1024,512]{1,0:T(8,128)(2,1)} %get-tuple-element.19) | copy-start | bytes 3145732
  213.0 2.3 collective-permute-start.3
  213.9 13.5 %collective-permute-start.10 = (bf16[512,512]{1,0:T(8,128)(2,1)S(1)}, bf16[512,512]{1,0:T(8,128)(2,1)S(1)}, u32[]{:S(2)}, u32[]{:S(2)}) collective-permute-start(bf16[512,512]{1,0:T(8,128)(2,1)S(1)} %add_convert_fusion.1), channel_id=1, source_target_pairs={{0,2},{2,0},{1,3},{3,1},{4,6},{6,4},{5,7},{7,5},{8,10},{10,8},{9,1... | collective-permute-start | bytes 1572872 | tf_op jit(solution)/shard_map/ppermute | solution.py:210
  216.4 22.2 %collective-permute-start.4 = (bf16[512,512]{1,0:T(8,128)(2,1)S(1)}, bf16[512,512]{1,0:T(8,128)(2,1)S(1)}, u32[]{:S(2)}, u32[]{:S(2)}) collective-permute-start(bf16[512,512]{1,0:T(8,128)(2,1)S(1)} %add_convert_fusion.5), channel_id=1, source_target_pairs={{0,2},{2,0},{1,3},{3,1},{4,6},{6,4},{5,7},{7,5},{8,10},{10,8},{9,1... | collective-permute-start | bytes 1572872 | tf_op jit(solution)/shard_map/ppermute | solution.py:210
  227.5 12.2 %collective-permute-start.11 = (bf16[512,512]{1,0:T(8,128)(2,1)S(1)}, bf16[512,512]{1,0:T(8,128)(2,1)S(1)}, u32[]{:S(2)}, u32[]{:S(2)}) collective-permute-start(bf16[512,512]{1,0:T(8,128)(2,1)S(1)} %add_convert_fusion), channel_id=1, source_target_pairs={{0,1},{1,0},{2,3},{3,2},{4,5},{5,4},{6,7},{7,6},{8,9},{9,8},{10,11... | collective-permute-start | bytes 1572872 | tf_op jit(solution)/shard_map/ppermute | solution.py:211
  238.8 2.5 collective-permute-start.5

commit v2 on v0

v2 whole, which is shorter than its diff:
```python
import functools

import jax
import jax.numpy as jnp
from jax import lax
from jax.experimental import pallas as pl
from jax.experimental.pallas import tpu as pltpu
from jax.sharding import PartitionSpec as P


LANES = 128
SUBLANES = 8
PIECES = (2, 2)
VMEM = 60 << 20
CORE = [(0, 1), (1, 0), (2, 3), (3, 2)]
CHIP = [(0, 2), (2, 0), (1, 3), (3, 1)]
F32 = jnp.float32
BF16 = jnp.bfloat16


def cost(flops, moved):
    return pl.CostEstimate(flops=flops, bytes_accessed=moved, transcendentals=0)


def lookup_kernel(layout, place, ids, tables, out, wide, evens, odds, id_evens, id_odds, sems):
    share, stride, offset, part = layout
    slots, rows, _ = tables.shape
    step = pl.program_id(0)
    steps = pl.num_programs(0)

    def fetch(destination, which):
        start = destination * stride + place[0] * share + offset
        return pltpu.make_async_copy(
            ids.at[:, pl.ds(pl.multiple_of(start, LANES), part)],
            (id_evens, id_odds)[which],
            sems.at[which],
        )

    @pl.when(step == 0)
    def _():
        fetch(0, 0).start()
        fetch(1, 1).start()
        for slot in range(slots):
            wide[pl.ds(slot * rows, rows), :] = tables[slot].astype(F32)

    for which in range(2):
        known = (id_evens, id_odds)[which]
        fetch(2 * step + which, which).wait()
        for slot in range(slots):
            for group in range(part // LANES):
                held = (evens, odds)[(slot * (part // LANES) + group) % 2]
                for row in range(LANES):
                    index = known[slot, group * LANES + row] + slot * rows
                    held[pl.ds(row, 1), :] = wide[pl.ds(index, 1), :]
                turned = held[...].T.astype(BF16)
                out[which, :, slot, :, group * LANES : (group + 1) * LANES] = turned.reshape(
                    out.shape[1], out.shape[3], LANES
                )

        @pl.when(step + 1 < steps)
        def _():
            fetch(2 * step + 2 + which, which).start()


def looked_up(ids, tables, place, sources, groups, share, offset, part):
    slots, rows, emb = tables.shape
    count = sources * slots * part
    return pl.pallas_call(
        functools.partial(lookup_kernel, (share, groups * share, offset, part)),
        grid_spec=pltpu.PrefetchScalarGridSpec(
            num_scalar_prefetch=1,
            grid=(sources // 2,),
            in_specs=[
                pl.BlockSpec(memory_space=pltpu.HBM),
                pl.BlockSpec((slots, rows, emb), lambda i, place: (0, 0, 0)),
            ],
            out_specs=pl.BlockSpec(
                (2, groups, slots, emb // groups, part), lambda i, place: (i, 0, 0, 0, 0)
            ),
            scratch_shapes=[
                pltpu.VMEM((slots * rows, emb), F32),
                pltpu.VMEM((LANES, emb), F32),
                pltpu.VMEM((LANES, emb), F32),
                pltpu.SMEM((slots, part), jnp.int32),
                pltpu.SMEM((slots, part), jnp.int32),
                pltpu.SemaphoreType.DMA((2,)),
            ],
        ),
        out_shape=jax.ShapeDtypeStruct((sources, groups, slots, emb // groups, part), BF16),
        cost_estimate=cost(count * 1_000_000, count * emb * 2),
        compiler_params=pltpu.CompilerParams(vmem_limit_bytes=VMEM),
        name="lookup",
    )(place, ids, tables)


def first_kernel(moved, placing, down, embedded, product, turned):
    _, many, _, emb, part = moved.shape
    wide = placing.shape[1]
    for inner in range(emb // SUBLANES):
        for group in range(many):
            for piece in range(part // LANES):
                block = moved[
                    :,
                    group,
                    :,
                    inner * SUBLANES : (inner + 1) * SUBLANES,
                    piece * LANES : (piece + 1) * LANES,
                ]
                at = (group * (part // LANES) + piece) * LANES
                turned[at : at + LANES, :] = (
                    block.astype(F32).reshape(wide, LANES).T.astype(BF16)
                )
        embedded[:, inner * wide : (inner + 1) * wide] = jnp.dot(
            turned[...], placing[...], preferred_element_type=F32
        ).astype(BF16)
    product[...] = jnp.dot(embedded[...], down[0], preferred_element_type=F32).astype(BF16)


def first(moved, placing, down, rows_each):
    sources, groups, slots, emb, part = moved.shape
    wide = placing.shape[0]
    width = sources * slots * emb
    rank = down.shape[2]
    rows = groups * part
    many = rows_each // part
    return pl.pallas_call(
        first_kernel,
        grid=(groups // many,),
        in_specs=[
            pl.BlockSpec((sources, many, slots, emb, part), lambda i: (0, i, 0, 0, 0)),
            pl.BlockSpec((wide, wide), lambda i: (0, 0)),
            pl.BlockSpec((1, width, rank), lambda i: (0, 0, 0)),
        ],
        out_specs=[
            pl.BlockSpec((rows_each, width), lambda i: (i, 0)),
            pl.BlockSpec((rows_each, rank), lambda i: (i, 0)),
        ],
        scratch_shapes=[pltpu.VMEM((rows_each, wide), BF16)],
        out_shape=[
            jax.ShapeDtypeStruct((rows, width), BF16),
            jax.ShapeDtypeStruct((rows, rank), BF16),
        ],
        cost_estimate=cost(4 * rows * width * rank, 4 * rows * width),
        compiler_params=pltpu.CompilerParams(vmem_limit_bytes=VMEM),
        name="first",
    )(moved, placing, down)


def low_of(place, mine, near, far, across):
    own = pl.program_id(0) == place[0] % 2
    pair = (mine[...].astype(F32) + near[...].astype(F32)).astype(BF16).astype(F32)
    other = jnp.where(own, far[...].astype(F32), across[...].astype(F32))
    return (pair + other).astype(BF16)


def middle_kernel(place, mine, near, far, across, embedded, up, bias, down, state, product):
    low = low_of(place, mine, near, far, across)
    width = embedded.shape[1]
    tile = 512
    for at in range(0, width, tile):
        cut = slice(at, at + tile)
        high = jnp.dot(low, up[0, :, cut], preferred_element_type=F32) + bias[0:1, cut]
        own = embedded[:, cut].astype(F32)
        state[:, cut] = (own * high + own).astype(BF16)
    product[...] = jnp.dot(state[...], down[0], preferred_element_type=F32).astype(BF16)


def low_specs(half, rank):
    return [
        pl.BlockSpec((half, rank), lambda i, place: (i, 0)),
        pl.BlockSpec((half, rank), lambda i, place: (i, 0)),
        pl.BlockSpec((half, rank), lambda i, place: (0, 0)),
        pl.BlockSpec((half, rank), lambda i, place: (0, 0)),
    ]


def middle(place, lows, embedded, up, bias, down, layer):
    rows, width = embedded.shape
    rank = up.shape[1]
    half = rows // 2
    return pl.pallas_call(
        middle_kernel,
        grid_spec=pltpu.PrefetchScalarGridSpec(
            num_scalar_prefetch=1,
            grid=(2,),
            in_specs=low_specs(half, rank)
            + [
                pl.BlockSpec((half, width), lambda i, place: (i, 0)),
                pl.BlockSpec((1, rank, width), lambda i, place: (layer, 0, 0)),
                pl.BlockSpec((1, width), lambda i, place: (0, 0)),
                pl.BlockSpec((1, width, rank), lambda i, place: (layer + 1, 0, 0)),
            ],
            out_specs=[
                pl.BlockSpec((half, width), lambda i, place: (i, 0)),
                pl.BlockSpec((half, rank), lambda i, place: (i, 0)),
            ],
        ),
        out_shape=[
            jax.ShapeDtypeStruct((rows, width), BF16),
            jax.ShapeDtypeStruct((rows, rank), BF16),
        ],
        cost_estimate=cost(4 * rows * width * rank, 4 * rows * width),
        compiler_params=pltpu.CompilerParams(vmem_limit_bytes=VMEM),
        name="middle",
    )(place, *lows, embedded, up, bias, down)


def last_kernel(place, mine, near, far, across, embedded, state, up, bias, *rest):
    out = rest[-1]
    low = low_of(place, mine, near, far, across)
    width = embedded.shape[1]
    groups, part = out.shape[0], out.shape[2]
    tile = 512
    for at in range(0, width, tile):
        cut = slice(at, at + tile)
        high = jnp.dot(low, up[0, :, cut], preferred_element_type=F32) + bias[0:1, cut]
        new = (
            embedded[:, cut].astype(F32) * high + state[:, cut].astype(F32)
        ).astype(BF16)
        out[:, 0, :, cut] = new.reshape(groups, part, tile)


def last(place, lows, embedded, state, up, bias, layer, so_far, groups, offset, part, share):
    rows, width = embedded.shape
    rank = up.shape[1]
    half = rows // 2
    in_specs = low_specs(half, rank) + [
        pl.BlockSpec((half, width), lambda i, place: (i, 0)),
        pl.BlockSpec((half, width), lambda i, place: (i, 0)),
        pl.BlockSpec((1, rank, width), lambda i, place: (layer, 0, 0)),
        pl.BlockSpec((1, width), lambda i, place: (0, 0)),
    ]
    args = [place, *lows, embedded, state, up, bias]
    aliases = {}
    if so_far is not None:
        in_specs.append(pl.BlockSpec(memory_space=pltpu.HBM))
        args.append(so_far)
        aliases = {9: 0}
    return pl.pallas_call(
        last_kernel,
        grid_spec=pltpu.PrefetchScalarGridSpec(
            num_scalar_prefetch=1,
            grid=(2,),
            in_specs=in_specs,
            out_specs=pl.BlockSpec(
                (groups // 2, 1, part, width), lambda i, place: (i, 0, offset // part, 0)
            ),
        ),
        out_shape=jax.ShapeDtypeStruct((groups, 1, share, width), BF16),
        input_output_aliases=aliases,
        cost_estimate=cost(2 * rows * width * rank, 6 * rows * width),
        compiler_params=pltpu.CompilerParams(vmem_limit_bytes=VMEM),
        name="last",
    )(*args)


def summed(product):
    half = product.shape[0] // 2
    start = lax.rem(lax.axis_index("mp"), 2) * half
    near = lax.ppermute(product, "mp", CORE)
    pair = (
        lax.dynamic_slice_in_dim(product, start, half, 0).astype(F32)
        + lax.dynamic_slice_in_dim(near, start, half, 0).astype(F32)
    ).astype(BF16)
    far = lax.ppermute(pair, "mp", CHIP)
    across = lax.ppermute(far, "mp", CORE)
    return product, near, far, across


def per_device(lookup_ids, table_feature, tables, cross_down, cross_up, cross_bias):
    feats = table_feature.shape[0]
    sources = lax.axis_size("batch")
    groups = lax.axis_size("mp")
    total = lookup_ids.shape[1] // sources
    share = total // groups
    place = lax.axis_index("mp").reshape(1).astype(jnp.int32)
    same = table_feature[:, None] == jnp.arange(feats, dtype=jnp.int32)[None, :]
    row = jnp.arange(SUBLANES, dtype=jnp.int32)
    placing = (
        (same[:, None, None, :] & (row[:, None] == row[None, :])[None, :, :, None])
        .astype(BF16)
        .reshape(feats * SUBLANES, SUBLANES * feats)
    )
    out = None
    unit = share // sum(PIECES)
    parts = [piece * unit for piece in PIECES]
    offset = 0
    for part in parts:
        looked = looked_up(
            lookup_ids, tables, place, sources, groups, share, offset, part
        )
        shape = looked.shape
        moved = lax.all_to_all(
            looked.reshape(sources * groups, *shape[2:]),
            ("batch", "mp"),
            0,
            0,
            tiled=True,
        ).reshape(shape)
        embedded, product = first(moved, placing, cross_down, groups * part // 2)
        lows = summed(product)
        state, product = middle(place, lows, embedded, cross_up, cross_bias[:1], cross_down, 0)
        lows = summed(product)
        out = last(
            place,
            lows,
            embedded,
            state,
            cross_up,
            cross_bias[1:],
            1,
            out,
            groups,
            offset,
            part,
            share,
        )
        offset += part
    return out.reshape(total, -1)


def solution(mesh):
    return jax.shard_map(
        per_device,
        mesh=mesh,
        in_specs=(
            P("batch", None),
            P(),
            P("batch", None, None),
            P(None, "mp", None),
            P(None, None, "mp"),
            P(None, "mp"),
        ),
        out_specs=P("batch", "mp"),
        check_vma=False,
    )
```

time: 465 us -> 247 us (0.53)
  blocking collectives: 194 us -> 0 us
  local copies, waits for them, and re-layouts: 179 us -> 5.18 us
  waiting for transfers between devices: 12.3 us -> 116 us
  Pallas kernels: 0 us -> 92.6 us
  matrix products: 42.3 us -> 0 us
  other arithmetic: 30.7 us -> 4.83 us
  starting transfers between devices: 4.61 us -> 26.5 us
    all_to_all x4 -> x0, blocking collectives: 194 us -> none  [the longest x1 109 us: one_exchange(): parts = lax.all_to_all(parts, axis, split_axis=0, concat_axis=0, tiled=True)]
    gather x2 -> x0, local copies, waits for them, and re-layouts: 115 us -> none  [per_device(): jnp.take(tables[slot], wanted[slot].reshape(sources * share), axis=0)]
    pallas_call x0 -> x8, Pallas kernels: none -> 92.6 us  [the longest x2 41 us: looked_up(): pl.pallas_call(functools.partial(lookup_kernel, (share, groups * share, o...]
    all_to_all x1 -> x2, waiting for transfers between devices: 12.3 us -> 73.6 us  [per_device(): lax.all_to_all(looked.reshape(sources * groups, *shape[2:]), ('batch', 'm...]
    dot_general x5 -> x0, matrix products: 42.3 us -> none  [the longest x2 19.3 us: per_device(): jnp.dot(low, cross_up[layer], preferred_element_type=jnp.float32)]
    ppermute x0 -> x12, waiting for transfers between devices: none -> 42.1 us  [the longest x4 39.2 us: summed(): far = lax.ppermute(pair, 'mp', CHIP)]
    select_n x2 -> x0, other arithmetic: 23 us -> none  [per_device(): jnp.take(tables[slot], wanted[slot].reshape(sources * share), axis=0)]
    reshape x2 -> x0, local copies, waits for them, and re-layouts: 20.5 us -> none  [the longest x1 12.4 us: per_device(): ordered.astype(jnp.bfloat16).reshape(examples_local, emb_local * feats)]
  transfers between devices with their start and end apart: 1 -> 14, of which waited for: 1 -> 8; matrix products, arithmetic and copies ran while one was open for 3% -> 3% of each run, Pallas kernels for 0% -> 26%
where the time goes in v2:
time: 247 us; the launch traced here: 245 us
  waiting for transfers between devices  116 us (47%)
  Pallas kernels  92.6 us (37%)
  starting transfers between devices  26.5 us (11%)
  local copies, waits for them, and re-layouts  5.18 us (2%)
  other arithmetic  4.83 us (2%)
    all_to_all x2, waiting for transfers between devices, per_device(): lax.all_to_all(looked.reshape(sources * groups, *shape[2:]), ('batch', 'm...  73.6 us
    pallas_call x2, Pallas kernels, looked_up(): pl.pallas_call(functools.partial(lookup_kernel, (share, groups * share, o...  41 us
    ppermute x4, waiting for transfers between devices, summed(): far = lax.ppermute(pair, 'mp', CHIP)  39.2 us
    pallas_call x2, Pallas kernels, middle(): pl.pallas_call(middle_kernel, grid_spec=pltpu.PrefetchScalarGridSpec(num_...  19.3 us
    all_to_all x2, starting transfers between devices, per_device(): lax.all_to_all(looked.reshape(sources * groups, *shape[2:]), ('batch', 'm...  17.6 us
    pallas_call x2, Pallas kernels, last(): pl.pallas_call(last_kernel, grid_spec=pltpu.PrefetchScalarGridSpec(num_sc...  16.2 us
    pallas_call x2, Pallas kernels, first(): pl.pallas_call(first_kernel, grid=(groups // many,), in_specs=[pl.BlockSp...  16.1 us
  transfers between devices with their start and end apart: 14, of which 8 were waited for; matrix products, arithmetic and copies ran while one was open for 3% of the time, Pallas kernels for 26%

profile of v2, /device:TPU:1, one launch (start us, length us, event | category | flops | bytes accessed | tf_op | source)
XLA Modules:
  0.0 245.0 jit_solution(12857602253915370238)
XLA Ops:
  0.0 20.5 %lookup.3 = bf16[32,4,2,32,256]{4,3,2,1,0:T(8,128)(2,1)} custom-call(s32[1]{0:T(128)} %bitcast.place, s32[2,65536]{1,0:T(2,128)} %ids.3, bf16[2,8192,128]{2,1,0:T(8,128)(2,1)} %tables.3), custom_call_target="tpu_custom_call" | custom-call | flops 16384000000 | bytes 4194304 | tf_op jit(solution)/shard_map/lookup/pallas_call | solution.py:68
  20.5 11.9 %all-to-all-start.1 = ((bf16[128,2,32,256]{3,2,1,0:T(8,128)(2,1)}), bf16[128,2,32,256]{3,2,1,0:T(8,128)(2,1)}, u32[]{:S(2)}, u32[]{:S(2)}) async-start(bf16[128,2,32,256]{3,2,1,0:T(8,128)(2,1)} %bitcast.9), calls=%async_computation.1 | async-start | bytes 8388608 | tf_op jit(solution)/shard_map/all_to_all | solution.py:293
  32.4 20.5 %lookup.2 = bf16[32,4,2,32,256]{4,3,2,1,0:T(8,128)(2,1)} custom-call(s32[1]{0:T(128)} %bitcast.place, s32[2,65536]{1,0:T(2,128)} %ids.3, bf16[2,8192,128]{2,1,0:T(8,128)(2,1)} %tables.3), custom_call_target="tpu_custom_call" | custom-call | flops 16384000000 | bytes 4194304 | tf_op jit(solution)/shard_map/lookup/pallas_call | solution.py:68
  52.9 32.1 %all-to-all-done.1 = bf16[128,2,32,256]{3,2,1,0:T(8,128)(2,1)} async-done(((bf16[128,2,32,256]{3,2,1,0:T(8,128)(2,1)}), bf16[128,2,32,256]{3,2,1,0:T(8,128)(2,1)}, u32[]{:S(2)}, u32[]{:S(2)}) %all-to-all-start.1) | async-done | bytes 4194336 | tf_op jit(solution)/shard_map/all_to_all | solution.py:293
  85.0 5.6 %all-to-all-start = ((bf16[128,2,32,256]{3,2,1,0:T(8,128)(2,1)}), bf16[128,2,32,256]{3,2,1,0:T(8,128)(2,1)}, u32[]{:S(2)}, u32[]{:S(2)}) async-start(bf16[128,2,32,256]{3,2,1,0:T(8,128)(2,1)} %bitcast.8), calls=%async_computation | async-start | bytes 8388608 | tf_op jit(solution)/shard_map/all_to_all | solution.py:293
  90.7 0.1 iota_compare_fusion
  90.8 0.4 and_convert_fusion
  91.1 1.4 reshape.60.placing
  92.5 8.0 %first.3 = (bf16[1024,2048]{1,0:T(8,128)(2,1)}, bf16[1024,512]{1,0:T(8,128)(2,1)}) custom-call(bf16[32,4,2,32,256]{4,3,2,1,0:T(8,128)(2,1)} %bitcast.4.moved, bf16[512,512]{1,0:T(8,128)(2,1)} %reshape.60.placing, bf16[2,2048,512]{2,1,0:T(8,128)(2,1)} %down.7), custom_call_target="tpu_custom_call" | custom-call | flops 4294967296 | bytes 8388608 | tf_op jit(solution)/shard_map/first/pallas_call | solution.py:126
  100.6 1.3 collective-permute-start.6
  101.8 41.5 %all-to-all-done = bf16[128,2,32,256]{3,2,1,0:T(8,128)(2,1)} async-done(((bf16[128,2,32,256]{3,2,1,0:T(8,128)(2,1)}), bf16[128,2,32,256]{3,2,1,0:T(8,128)(2,1)}, u32[]{:S(2)}, u32[]{:S(2)}) %all-to-all-start) | async-done | bytes 4194336 | tf_op jit(solution)/shard_map/all_to_all | solution.py:293
  143.4 8.1 %first.2 = (bf16[1024,2048]{1,0:T(8,128)(2,1)}, bf16[1024,512]{1,0:T(8,128)(2,1)}) custom-call(bf16[32,4,2,32,256]{4,3,2,1,0:T(8,128)(2,1)} %bitcast.2.moved, bf16[512,512]{1,0:T(8,128)(2,1)} %reshape.60.placing, bf16[2,2048,512]{2,1,0:T(8,128)(2,1)} %down.7), custom_call_target="tpu_custom_call" | custom-call | flops 4294967296 | bytes 8388608 | tf_op jit(solution)/shard_map/first/pallas_call | solution.py:126
  151.5 1.0 collective-permute-start
  152.4 0.0 collective-permute-done.6.near
  152.5 1.2 add_convert_fusion.1
  153.6 0.4 collective-permute-start.7
  154.0 0.9 collective-permute-done.near
  154.9 1.5 add_convert_fusion.3
  156.5 0.4 collective-permute-start.1
  156.9 10.3 %collective-permute-done.7.far = bf16[512,512]{1,0:T(8,128)(2,1)S(1)} collective-permute-done((bf16[512,512]{1,0:T(8,128)(2,1)S(1)}, bf16[512,512]{1,0:T(8,128)(2,1)S(1)}, u32[]{:S(2)}, u32[]{:S(2)}) %collective-permute-start.7) | collective-permute-done | bytes 524320 | tf_op jit(solution)/shard_map/ppermute | solution.py:265
  167.2 1.4 collective-permute-start.8
  168.5 9.9 %collective-permute-done.1.far = bf16[512,512]{1,0:T(8,128)(2,1)S(1)} collective-permute-done((bf16[512,512]{1,0:T(8,128)(2,1)S(1)}, bf16[512,512]{1,0:T(8,128)(2,1)S(1)}, u32[]{:S(2)}, u32[]{:S(2)}) %collective-permute-start.1) | collective-permute-done | bytes 524320 | tf_op jit(solution)/shard_map/ppermute | solution.py:265
  178.4 0.9 collective-permute-start.2
  179.3 0.6 fusion
  179.9 0.0 collective-permute-done.8.across
  179.9 0.8 copy-done.14
  180.7 9.6 %middle.3 = (bf16[1024,2048]{1,0:T(8,128)(2,1)}, bf16[1024,512]{1,0:T(8,128)(2,1)}) custom-call(s32[1]{0:T(128)} %bitcast.place, bf16[1024,512]{1,0:T(8,128)(2,1)} %get-tuple-element.17.mine, bf16[1024,512]{1,0:T(8,128)(2,1)} %collective-permute-done.6.near, bf16[512,512]{1,0:T(8,128)(2,1)} %copy-done.12, bf16[512,512]{1,0:T(8,128)(2,1)} %copy-done.14, ...), custom_call_target="tpu_custom_call" | custom-call | flops 4294967296 | bytes 8388608 | tf_op jit(solution)/shard_map/middle/pallas_call | solution.py:181
  190.3 0.1 collective-permute-start.9
  190.5 0.0 collective-permute-done.2.across
  190.5 0.8 copy-done.13
  191.2 9.7 %middle.2 = (bf16[1024,2048]{1,0:T(8,128)(2,1)}, bf16[1024,512]{1,0:T(8,128)(2,1)}) custom-call(s32[1]{0:T(128)} %bitcast.place, bf16[1024,512]{1,0:T(8,128)(2,1)} %get-tuple-element.13.mine, bf16[1024,512]{1,0:T(8,128)(2,1)} %copy-done.8, bf16[512,512]{1,0:T(8,128)(2,1)} %copy-done.11, bf16[512,512]{1,0:T(8,128)(2,1)} %copy-done.13, ...), custom_call_target="tpu_custom_call" | custom-call | flops 4294967296 | bytes 8388608 | tf_op jit(solution)/shard_map/middle/pallas_call | solution.py:181
  201.0 0.4 collective-permute-start.3
  201.4 0.0 collective-permute-done.9.near
  201.4 0.1 add_convert_fusion
  201.6 0.4 collective-permute-start.10
  201.9 2.0 collective-permute-done.3.near
  203.9 1.5 add_convert_fusion.2
  205.4 0.4 collective-permute-start.4
  205.8 9.2 %collective-permute-done.10.far = bf16[512,512]{1,0:T(8,128)(2,1)S(1)} collective-permute-done((bf16[512,512]{1,0:T(8,128)(2,1)S(1)}, bf16[512,512]{1,0:T(8,128)(2,1)S(1)}, u32[]{:S(2)}, u32[]{:S(2)}) %collective-permute-start.10) | collective-permute-done | bytes 524320 | tf_op jit(solution)/shard_map/ppermute | solution.py:265
  215.1 1.4 collective-permute-start.11
  216.5 9.8 %collective-permute-done.4.far = bf16[512,512]{1,0:T(8,128)(2,1)S(1)} collective-permute-done((bf16[512,512]{1,0:T(8,128)(2,1)S(1)}, bf16[512,512]{1,0:T(8,128)(2,1)S(1)}, u32[]{:S(2)}, u32[]{:S(2)}) %collective-permute-start.4) | collective-permute-done | bytes 524320 | tf_op jit(solution)/shard_map/ppermute | solution.py:265
  226.3 0.9 collective-permute-start.5
  227.2 0.0 collective-permute-done.11.across
  227.2 0.8 copy-done.6
  228.0 8.1 %last.2.rest_0_ = bf16[4,1,512,2048]{3,2,1,0:T(8,128)(2,1)} custom-call(s32[1]{0:T(128)} %bitcast.place, bf16[1024,512]{1,0:T(8,128)(2,1)} %get-tuple-element.19.mine, bf16[1024,512]{1,0:T(8,128)(2,1)} %copy-done.1, bf16[512,512]{1,0:T(8,128)(2,1)} %copy-done.5, bf16[512,512]{1,0:T(8,128)(2,1)} %copy-done.6, bf16[1024,2048]{1,0:T(8,128)(2,1)} %get-tuple-element.18.embedded, ...), custom_call_target="tpu_custom_call" | custom-call | flops 2147483648 | bytes 12582912 | tf_op jit(solution)/shard_map/last/pallas_call | solution.py:239
  236.1 0.0 collective-permute-done.5.across
  236.1 0.8 copy-done.4
  236.9 8.1 %last.3 = bf16[4,1,512,2048]{3,2,1,0:T(8,128)(2,1)} custom-call(s32[1]{0:T(128)} %bitcast.place, bf16[1024,512]{1,0:T(8,128)(2,1)} %get-tuple-element.15.mine, bf16[1024,512]{1,0:T(8,128)(2,1)} %copy-done.2, bf16[512,512]{1,0:T(8,128)(2,1)} %copy-done.3, bf16[512,512]{1,0:T(8,128)(2,1)} %copy-done.4, ...), custom_call_target="tpu_custom_call", output_to_operand_aliasing={{}: (9, {})} | custom-call | flops 2147483648 | bytes 12582912 | tf_op jit(solution)/shard_map/last/pallas_call | solution.py:239
  (27 shorter events, 0.1 us)
Async XLA Ops:
  20.5 64.5 %all-to-all-start.1 = ((bf16[128,2,32,256]{3,2,1,0:T(8,128)(2,1)}), bf16[128,2,32,256]{3,2,1,0:T(8,128)(2,1)}, u32[]{:S(2)}, u32[]{:S(2)}) async-start(bf16[128,2,32,256]{3,2,1,0:T(8,128)(2,1)} %bitcast.9), calls=%async_computation.1 | async-start | bytes 8388608 | tf_op jit(solution)/shard_map/all_to_all | solution.py:293
  85.0 5.7 %copy-start.10 = (s32[64]{0:T(128)S(1)}, s32[64]{0:T(128)}, u32[]{:S(2)}) copy-start(s32[64]{0:T(128)} %param.7) | copy-start | bytes 772
  85.0 58.4 %all-to-all-start = ((bf16[128,2,32,256]{3,2,1,0:T(8,128)(2,1)}), bf16[128,2,32,256]{3,2,1,0:T(8,128)(2,1)}, u32[]{:S(2)}, u32[]{:S(2)}) async-start(bf16[128,2,32,256]{3,2,1,0:T(8,128)(2,1)} %bitcast.8), calls=%async_computation | async-start | bytes 8388608 | tf_op jit(solution)/shard_map/all_to_all | solution.py:293
  100.6 51.9 %collective-permute-start.6 = (bf16[1024,512]{1,0:T(8,128)(2,1)}, bf16[1024,512]{1,0:T(8,128)(2,1)}, u32[]{:S(2)}, u32[]{:S(2)}) collective-permute-start(bf16[1024,512]{1,0:T(8,128)(2,1)} %get-tuple-element.17.mine), channel_id=1, source_target_pairs={{0,1},{1,0},{2,3},{3,2},{4,5},{5,4},{6,7},{7,6},{8,9},{9,8},{10,11... | collective-permute-start | bytes 3145736 | tf_op jit(solution)/shard_map/ppermute | solution.py:260
  143.4 9.1 %copy-start.7 = (bf16[1024,512]{1,0:T(8,128)(2,1)S(1)}, bf16[1024,512]{1,0:T(8,128)(2,1)}, u32[]{:S(2)}) copy-start(bf16[1024,512]{1,0:T(8,128)(2,1)} %get-tuple-element.17.mine) | copy-start | bytes 3145732
  143.4 35.9 %copy-start.9 = (f32[2,2048]{1,0:T(2,128)S(1)}, f32[2,2048]{1,0:T(2,128)}, u32[]{:S(2)}) copy-start(f32[2,2048]{1,0:T(2,128)} %param.11) | copy-start | bytes 49156
  151.5 3.5 %collective-permute-start = (bf16[1024,512]{1,0:T(8,128)(2,1)}, bf16[1024,512]{1,0:T(8,128)(2,1)S(1)}, u32[]{:S(2)}, u32[]{:S(2)}) collective-permute-start(bf16[1024,512]{1,0:T(8,128)(2,1)} %get-tuple-element.13.mine), channel_id=1, source_target_pairs={{0,1},{1,0},{2,3},{3,2},{4,5},{5,4},{6,7},{7,6},{8,9},{9,8},{10,11... | collective-permute-start | bytes 3145736 | tf_op jit(solution)/shard_map/ppermute | solution.py:260
  153.6 13.5 %collective-permute-start.7 = (bf16[512,512]{1,0:T(8,128)(2,1)S(1)}, bf16[512,512]{1,0:T(8,128)(2,1)S(1)}, u32[]{:S(2)}, u32[]{:S(2)}) collective-permute-start(bf16[512,512]{1,0:T(8,128)(2,1)S(1)} %add_convert_fusion.1), channel_id=1, source_target_pairs={{0,2},{2,0},{1,3},{3,1},{4,6},{6,4},{5,7},{7,5},{8,10},{10,8},{9,1... | collective-permute-start | bytes 1572872 | tf_op jit(solution)/shard_map/ppermute | solution.py:265
  154.9 35.4 %copy-start.8 = (bf16[1024,512]{1,0:T(8,128)(2,1)}, bf16[1024,512]{1,0:T(8,128)(2,1)S(1)}, u32[]{:S(2)}) copy-start(bf16[1024,512]{1,0:T(8,128)(2,1)S(1)} %collective-permute-done.near) | copy-start | bytes 3145732
  156.5 21.9 %collective-permute-start.1 = (bf16[512,512]{1,0:T(8,128)(2,1)S(1)}, bf16[512,512]{1,0:T(8,128)(2,1)S(1)}, u32[]{:S(2)}, u32[]{:S(2)}) collective-permute-start(bf16[512,512]{1,0:T(8,128)(2,1)S(1)} %add_convert_fusion.3), channel_id=1, source_target_pairs={{0,2},{2,0},{1,3},{3,1},{4,6},{6,4},{5,7},{7,5},{8,10},{10,8},{9,1... | collective-permute-start | bytes 1572872 | tf_op jit(solution)/shard_map/ppermute | solution.py:265
  167.2 12.7 %copy-start.12 = (bf16[512,512]{1,0:T(8,128)(2,1)}, bf16[512,512]{1,0:T(8,128)(2,1)S(1)}, u32[]{:S(2)}) copy-start(bf16[512,512]{1,0:T(8,128)(2,1)S(1)} %collective-permute-done.7.far) | copy-start | bytes 1572868
  167.2 12.7 %collective-permute-start.8 = (bf16[512,512]{1,0:T(8,128)(2,1)S(1)}, bf16[512,512]{1,0:T(8,128)(2,1)S(1)}, u32[]{:S(2)}, u32[]{:S(2)}) collective-permute-start(bf16[512,512]{1,0:T(8,128)(2,1)S(1)} %collective-permute-done.7.far), channel_id=1, source_target_pairs={{0,1},{1,0},{2,3},{3,2},{4,5},{5,4},{6,7},{7,6},{8,9},{9,8},{10,11... | collective-permute-start | bytes 1572872 | tf_op jit(solution)/shard_map/ppermute | solution.py:266
  178.4 11.9 %copy-start.11 = (bf16[512,512]{1,0:T(8,128)(2,1)}, bf16[512,512]{1,0:T(8,128)(2,1)S(1)}, u32[]{:S(2)}) copy-start(bf16[512,512]{1,0:T(8,128)(2,1)S(1)} %collective-permute-done.1.far) | copy-start | bytes 1572868
  178.4 12.0 %collective-permute-start.2 = (bf16[512,512]{1,0:T(8,128)(2,1)S(1)}, bf16[512,512]{1,0:T(8,128)(2,1)S(1)}, u32[]{:S(2)}, u32[]{:S(2)}) collective-permute-start(bf16[512,512]{1,0:T(8,128)(2,1)S(1)} %collective-permute-done.1.far), channel_id=1, source_target_pairs={{0,1},{1,0},{2,3},{3,2},{4,5},{5,4},{6,7},{7,6},{8,9},{9,8},{10,11... | collective-permute-start | bytes 1572872 | tf_op jit(solution)/shard_map/ppermute | solution.py:266
  179.9 0.8 copy-start.14
  190.3 11.1 %collective-permute-start.9 = (bf16[1024,512]{1,0:T(8,128)(2,1)}, bf16[1024,512]{1,0:T(8,128)(2,1)S(1)}, u32[]{:S(2)}, u32[]{:S(2)}) collective-permute-start(bf16[1024,512]{1,0:T(8,128)(2,1)} %get-tuple-element.19.mine), channel_id=1, source_target_pairs={{0,1},{1,0},{2,3},{3,2},{4,5},{5,4},{6,7},{7,6},{8,9},{9,8},{10,11... | collective-permute-start | bytes 3145736 | tf_op jit(solution)/shard_map/ppermute | solution.py:260
  190.5 0.8 copy-start.13
  191.2 10.2 %copy-start = (bf16[1024,512]{1,0:T(8,128)(2,1)S(1)}, bf16[1024,512]{1,0:T(8,128)(2,1)}, u32[]{:S(2)}) copy-start(bf16[1024,512]{1,0:T(8,128)(2,1)} %get-tuple-element.19.mine) | copy-start | bytes 3145732
  201.0 2.9 %collective-permute-start.3 = (bf16[1024,512]{1,0:T(8,128)(2,1)}, bf16[1024,512]{1,0:T(8,128)(2,1)S(1)}, u32[]{:S(2)}, u32[]{:S(2)}) collective-permute-start(bf16[1024,512]{1,0:T(8,128)(2,1)} %get-tuple-element.15.mine), channel_id=1, source_target_pairs={{0,1},{1,0},{2,3},{3,2},{4,5},{5,4},{6,7},{7,6},{8,9},{9,8},{10,11... | collective-permute-start | bytes 3145736 | tf_op jit(solution)/shard_map/ppermute | solution.py:260
  201.4 26.6 %copy-start.1 = (bf16[1024,512]{1,0:T(8,128)(2,1)}, bf16[1024,512]{1,0:T(8,128)(2,1)S(1)}, u32[]{:S(2)}) copy-start(bf16[1024,512]{1,0:T(8,128)(2,1)S(1)} %collective-permute-done.9.near) | copy-start | bytes 3145732
  201.6 13.5 %collective-permute-start.10 = (bf16[512,512]{1,0:T(8,128)(2,1)S(1)}, bf16[512,512]{1,0:T(8,128)(2,1)S(1)}, u32[]{:S(2)}, u32[]{:S(2)}) collective-permute-start(bf16[512,512]{1,0:T(8,128)(2,1)S(1)} %add_convert_fusion), channel_id=1, source_target_pairs={{0,2},{2,0},{1,3},{3,1},{4,6},{6,4},{5,7},{7,5},{8,10},{10,8},{9,1... | collective-permute-start | bytes 1572872 | tf_op jit(solution)/shard_map/ppermute | solution.py:265
  203.9 32.2 %copy-start.2 = (bf16[1024,512]{1,0:T(8,128)(2,1)}, bf16[1024,512]{1,0:T(8,128)(2,1)S(1)}, u32[]{:S(2)}) copy-start(bf16[1024,512]{1,0:T(8,128)(2,1)S(1)} %collective-permute-done.3.near) | copy-start | bytes 3145732
  205.4 20.9 %collective-permute-start.4 = (bf16[512,512]{1,0:T(8,128)(2,1)S(1)}, bf16[512,512]{1,0:T(8,128)(2,1)S(1)}, u32[]{:S(2)}, u32[]{:S(2)}) collective-permute-start(bf16[512,512]{1,0:T(8,128)(2,1)S(1)} %add_convert_fusion.2), channel_id=1, source_target_pairs={{0,2},{2,0},{1,3},{3,1},{4,6},{6,4},{5,7},{7,5},{8,10},{10,8},{9,1... | collective-permute-start | bytes 1572872 | tf_op jit(solution)/shard_map/ppermute | solution.py:265
  215.1 13.0 %copy-start.5 = (bf16[512,512]{1,0:T(8,128)(2,1)}, bf16[512,512]{1,0:T(8,128)(2,1)S(1)}, u32[]{:S(2)}) copy-start(bf16[512,512]{1,0:T(8,128)(2,1)S(1)} %collective-permute-done.10.far) | copy-start | bytes 1572868
  215.1 12.2 %collective-permute-start.11 = (bf16[512,512]{1,0:T(8,128)(2,1)S(1)}, bf16[512,512]{1,0:T(8,128)(2,1)S(1)}, u32[]{:S(2)}, u32[]{:S(2)}) collective-permute-start(bf16[512,512]{1,0:T(8,128)(2,1)S(1)} %collective-permute-done.10.far), channel_id=1, source_target_pairs={{0,1},{1,0},{2,3},{3,2},{4,5},{5,4},{6,7},{7,6},{8,9},{9,8},{10,11... | collective-permute-start | bytes 1572872 | tf_op jit(solution)/shard_map/ppermute | solution.py:266
  226.3 9.8 %copy-start.3 = (bf16[512,512]{1,0:T(8,128)(2,1)}, bf16[512,512]{1,0:T(8,128)(2,1)S(1)}, u32[]{:S(2)}) copy-start(bf16[512,512]{1,0:T(8,128)(2,1)S(1)} %collective-permute-done.4.far) | copy-start | bytes 1572868
  226.3 9.8 %collective-permute-start.5 = (bf16[512,512]{1,0:T(8,128)(2,1)S(1)}, bf16[512,512]{1,0:T(8,128)(2,1)S(1)}, u32[]{:S(2)}, u32[]{:S(2)}) collective-permute-start(bf16[512,512]{1,0:T(8,128)(2,1)S(1)} %collective-permute-done.4.far), channel_id=1, source_target_pairs={{0,1},{1,0},{2,3},{3,2},{4,5},{5,4},{6,7},{7,6},{8,9},{9,8},{10,11... | collective-permute-start | bytes 1572872 | tf_op jit(solution)/shard_map/ppermute | solution.py:266
  227.2 0.8 copy-start.6
  236.1 0.8 copy-start.4

commit v3 on v2

--- a/solution.py
+++ b/solution.py
@@ -12,6 +12,7 @@
 SUBLANES = 8
 PIECES = (2, 2)
 VMEM = 60 << 20
+CROSS_VMEM = 24 << 20
 CORE = [(0, 1), (1, 0), (2, 3), (3, 2)]
 CHIP = [(0, 2), (2, 0), (1, 3), (3, 1)]
 F32 = jnp.float32
@@ -22,67 +23,87 @@
     return pl.CostEstimate(flops=flops, bytes_accessed=moved, transcendentals=0)
 
 
-def lookup_kernel(layout, place, ids, tables, out, wide, evens, odds, id_evens, id_odds, sems):
-    share, stride, offset, part = layout
+def lookup_kernel(layout, place, ids, tables, out, wide, evens, odds, staged, *rest):
+    share, stride, offset, part, width, sources = layout
+    known, sems, moved = rest[:2], rest[2], rest[3]
     slots, rows, _ = tables.shape
     step = pl.program_id(0)
     steps = pl.num_programs(0)
-
-    def fetch(destination, which):
+    run = width // 2 * part
+
+    def stage(destination):
         start = destination * stride + place[0] * share + offset
         return pltpu.make_async_copy(
             ids.at[:, pl.ds(pl.multiple_of(start, LANES), part)],
-            (id_evens, id_odds)[which],
-            sems.at[which],
+            staged.at[:, pl.ds(destination * part, part)],
+            sems.at[destination],
+        )
+
+    def fetch(at, which):
+        start = (2 * at + which) * run
+        return pltpu.make_async_copy(
+            staged.at[:, pl.ds(pl.multiple_of(start, LANES), run)], known[which], moved.at[which]
         )
 
     @pl.when(step == 0)
     def _():
-        fetch(0, 0).start()
-        fetch(1, 1).start()
+        for destination in range(sources):
+            stage(destination).start()
         for slot in range(slots):
             wide[pl.ds(slot * rows, rows), :] = tables[slot].astype(F32)
+        for destination in range(sources):
+            stage(destination).wait()
+        for which in range(2):
+            fetch(0, which).start()
 
     for which in range(2):
-        known = (id_evens, id_odds)[which]
-        fetch(2 * step + which, which).wait()
-        for slot in range(slots):
-            for group in range(part // LANES):
-                held = (evens, odds)[(slot * (part // LANES) + group) % 2]
-                for row in range(LANES):
-                    index = known[slot, group * LANES + row] + slot * rows
-                    held[pl.ds(row, 1), :] = wide[pl.ds(index, 1), :]
-                turned = held[...].T.astype(BF16)
-                out[which, :, slot, :, group * LANES : (group + 1) * LANES] = turned.reshape(
-                    out.shape[1], out.shape[3], LANES
-                )
+        fetch(step, which).wait()
+        for inner in range(width // 2):
+            for slot in range(slots):
+                for group in range(part // LANES):
+                    held = (evens, odds)[(slot * (part // LANES) + group) % 2]
+                    for row in range(LANES):
+                        index = known[which][slot, inner * part + group * LANES + row]
+                        held[pl.ds(row, 1), :] = wide[pl.ds(index + slot * rows, 1), :]
+                    turned = held[...].T.astype(BF16)
+                    out[
+                        which * (width // 2) + inner,
+                        :,
+                        slot,
+                        :,
+                        group * LANES : (group + 1) * LANES,
+                    ] = turned.reshape(out.shape[1], out.shape[3], LANES)
 
         @pl.when(step + 1 < steps)
         def _():
-            fetch(2 * step + 2 + which, which).start()
+            fetch(step + 1, which).start()
 
 
 def looked_up(ids, tables, place, sources, groups, share, offset, part):
     slots, rows, emb = tables.shape
     count = sources * slots * part
+    width = 8
+    layout = (share, groups * share, offset, part, width, sources)
     return pl.pallas_call(
-        functools.partial(lookup_kernel, (share, groups * share, offset, part)),
+        functools.partial(lookup_kernel, layout),
         grid_spec=pltpu.PrefetchScalarGridSpec(
             num_scalar_prefetch=1,
-            grid=(sources // 2,),
+            grid=(sources // width,),
             in_specs=[
                 pl.BlockSpec(memory_space=pltpu.HBM),
                 pl.BlockSpec((slots, rows, emb), lambda i, place: (0, 0, 0)),
             ],
             out_specs=pl.BlockSpec(
-                (2, groups, slots, emb // groups, part), lambda i, place: (i, 0, 0, 0, 0)
+                (width, groups, slots, emb // groups, part), lambda i, place: (i, 0, 0, 0, 0)
             ),
             scratch_shapes=[
                 pltpu.VMEM((slots * rows, emb), F32),
                 pltpu.VMEM((LANES, emb), F32),
                 pltpu.VMEM((LANES, emb), F32),
-                pltpu.SMEM((slots, part), jnp.int32),
-                pltpu.SMEM((slots, part), jnp.int32),
+                pltpu.VMEM((slots, sources * part), jnp.int32),
+                pltpu.SMEM((slots, width // 2 * part), jnp.int32),
+                pltpu.SMEM((slots, width // 2 * part), jnp.int32),
+                pltpu.SemaphoreType.DMA((sources,)),
                 pltpu.SemaphoreType.DMA((2,)),
             ],
         ),
@@ -141,7 +162,7 @@
             jax.ShapeDtypeStruct((rows, rank), BF16),
         ],
         cost_estimate=cost(4 * rows * width * rank, 4 * rows * width),
-        compiler_params=pltpu.CompilerParams(vmem_limit_bytes=VMEM),
+        compiler_params=pltpu.CompilerParams(vmem_limit_bytes=CROSS_VMEM),
         name="first",
     )(moved, placing, down)
 
@@ -200,7 +221,7 @@
             jax.ShapeDtypeStruct((rows, rank), BF16),
         ],
         cost_estimate=cost(4 * rows * width * rank, 4 * rows * width),
-        compiler_params=pltpu.CompilerParams(vmem_limit_bytes=VMEM),
+        compiler_params=pltpu.CompilerParams(vmem_limit_bytes=CROSS_VMEM),
         name="middle",
     )(place, *lows, embedded, up, bias, down)
 
@@ -249,7 +270,7 @@
         out_shape=jax.ShapeDtypeStruct((groups, 1, share, width), BF16),
         input_output_aliases=aliases,
         cost_estimate=cost(2 * rows * width * rank, 6 * rows * width),
-        compiler_params=pltpu.CompilerParams(vmem_limit_bytes=VMEM),
+        compiler_params=pltpu.CompilerParams(vmem_limit_bytes=CROSS_VMEM),
         name="last",
     )(*args)
 

time: 247 us -> 235 us (0.951)
  Pallas kernels: 92.6 us -> 70.9 us
  local copies, waits for them, and re-layouts: 5.18 us -> 15.5 us
    unnamed x30 -> x24, local copies, waits for them, and re-layouts: 3.17 us -> 14.9 us
    pallas_call x2, Pallas kernels: 16.2 us -> 9.15 us  [last(): pl.pallas_call(last_kernel, grid_spec=pltpu.PrefetchScalarGridSpec(num_sc...]
    pallas_call x2, Pallas kernels: 19.3 us -> 13 us  [middle(): pl.pallas_call(middle_kernel, grid_spec=pltpu.PrefetchScalarGridSpec(num_...]
    pallas_call x2, Pallas kernels: 41 us -> 35.9 us  [looked_up(): pl.pallas_call(functools.partial(lookup_kernel, layout), grid_spec=pltpu....]
    pallas_call x2, Pallas kernels: 16.1 us -> 12.8 us  [first(): pl.pallas_call(first_kernel, grid=(groups // many,), in_specs=[pl.BlockSp...]
  transfers between devices with their start and end apart: 14 -> 14, of which waited for: 8 -> 8; matrix products, arithmetic and copies ran while one was open for 3% -> 2% of each run, Pallas kernels for 26% -> 21%
where the time goes in v3:
time: 235 us
  waiting for transfers between devices  118 us (50%)
  Pallas kernels  70.9 us (30%)
  starting transfers between devices  26.5 us (11%)
  local copies, waits for them, and re-layouts  15.5 us (7%)
  other arithmetic  3.08 us (1%)
    all_to_all x2, waiting for transfers between devices, per_device(): lax.all_to_all(looked.reshape(sources * groups, *shape[2:]), ('batch', 'm...  74.4 us
    ppermute x4, waiting for transfers between devices, summed(): far = lax.ppermute(pair, 'mp', CHIP)  41.4 us
    pallas_call x2, Pallas kernels, looked_up(): pl.pallas_call(functools.partial(lookup_kernel, layout), grid_spec=pltpu....  35.9 us
    all_to_all x2, starting transfers between devices, per_device(): lax.all_to_all(looked.reshape(sources * groups, *shape[2:]), ('batch', 'm...  17.6 us
    unnamed x24, local copies, waits for them, and re-layouts  14.9 us
    pallas_call x2, Pallas kernels, middle(): pl.pallas_call(middle_kernel, grid_spec=pltpu.PrefetchScalarGridSpec(num_...  13 us
    pallas_call x2, Pallas kernels, first(): pl.pallas_call(first_kernel, grid=(groups // many,), in_specs=[pl.BlockSp...  12.8 us
    pallas_call x2, Pallas kernels, last(): pl.pallas_call(last_kernel, grid_spec=pltpu.PrefetchScalarGridSpec(num_sc...  9.15 us
  transfers between devices with their start and end apart: 14, of which 8 were waited for; matrix products, arithmetic and copies ran while one was open for 2% of the time, Pallas kernels for 21%

profile of v3, /device:TPU:1, one launch (start us, length us, event | category | flops | bytes accessed | tf_op | source)
XLA Modules:
  0.0 234.6 jit_solution(6227477041113526592)
XLA Ops:
  0.0 18.0 %lookup.3 = bf16[32,4,2,32,256]{4,3,2,1,0:T(8,128)(2,1)} custom-call(s32[1]{0:T(128)} %bitcast.place, s32[2,65536]{1,0:T(2,128)} %ids.3, bf16[2,8192,128]{2,1,0:T(8,128)(2,1)} %tables.3), custom_call_target="tpu_custom_call" | custom-call | flops 16384000000 | bytes 4194304 | tf_op jit(solution)/shard_map/lookup/pallas_call | solution.py:87
  18.0 11.9 %all-to-all-start.1 = ((bf16[128,2,32,256]{3,2,1,0:T(8,128)(2,1)}), bf16[128,2,32,256]{3,2,1,0:T(8,128)(2,1)}, u32[]{:S(2)}, u32[]{:S(2)}) async-start(bf16[128,2,32,256]{3,2,1,0:T(8,128)(2,1)} %bitcast.9), calls=%async_computation.1 | async-start | bytes 8388608 | tf_op jit(solution)/shard_map/all_to_all | solution.py:314
  29.9 17.9 %lookup.2 = bf16[32,4,2,32,256]{4,3,2,1,0:T(8,128)(2,1)} custom-call(s32[1]{0:T(128)} %bitcast.place, s32[2,65536]{1,0:T(2,128)} %ids.3, bf16[2,8192,128]{2,1,0:T(8,128)(2,1)} %tables.3), custom_call_target="tpu_custom_call" | custom-call | flops 16384000000 | bytes 4194304 | tf_op jit(solution)/shard_map/lookup/pallas_call | solution.py:87
  47.9 34.6 %all-to-all-done.1 = bf16[128,2,32,256]{3,2,1,0:T(8,128)(2,1)} async-done(((bf16[128,2,32,256]{3,2,1,0:T(8,128)(2,1)}), bf16[128,2,32,256]{3,2,1,0:T(8,128)(2,1)}, u32[]{:S(2)}, u32[]{:S(2)}) %all-to-all-start.1) | async-done | bytes 4194336 | tf_op jit(solution)/shard_map/all_to_all | solution.py:314
  82.5 5.7 %all-to-all-start = ((bf16[128,2,32,256]{3,2,1,0:T(8,128)(2,1)}), bf16[128,2,32,256]{3,2,1,0:T(8,128)(2,1)}, u32[]{:S(2)}, u32[]{:S(2)}) async-start(bf16[128,2,32,256]{3,2,1,0:T(8,128)(2,1)} %bitcast.8), calls=%async_computation | async-start | bytes 8388608 | tf_op jit(solution)/shard_map/all_to_all | solution.py:314
  88.2 0.1 iota_compare_fusion
  88.3 0.4 and_convert_fusion
  88.7 0.6 reshape.60.placing
  89.3 0.0 copy-start.7
  89.3 2.2 copy-done.7
  91.5 6.4 %first.3 = (bf16[1024,2048]{1,0:T(8,128)(2,1)S(1)}, bf16[1024,512]{1,0:T(8,128)(2,1)S(1)}) custom-call(bf16[32,4,2,32,256]{4,3,2,1,0:T(8,128)(2,1)} %bitcast.4.moved, bf16[512,512]{1,0:T(8,128)(2,1)S(1)} %reshape.60.placing, bf16[2,2048,512]{2,1,0:T(8,128)(2,1)S(1)} %copy-done.7), custom_call_target="tpu_custom_call" | custom-call | flops 4294967296 | bytes 8388608 | tf_op jit(solution)/shard_map/first/pallas_call | solution.py:147
  97.9 2.0 copy-done.2
  99.9 1.3 collective-permute-start.6
  101.1 39.8 %all-to-all-done = bf16[128,2,32,256]{3,2,1,0:T(8,128)(2,1)} async-done(((bf16[128,2,32,256]{3,2,1,0:T(8,128)(2,1)}), bf16[128,2,32,256]{3,2,1,0:T(8,128)(2,1)}, u32[]{:S(2)}, u32[]{:S(2)}) %all-to-all-start) | async-done | bytes 4194336 | tf_op jit(solution)/shard_map/all_to_all | solution.py:314
  140.9 2.2 copy-done.8
  143.1 6.4 %first.2 = (bf16[1024,2048]{1,0:T(8,128)(2,1)S(1)}, bf16[1024,512]{1,0:T(8,128)(2,1)S(1)}) custom-call(bf16[32,4,2,32,256]{4,3,2,1,0:T(8,128)(2,1)} %bitcast.2.moved, bf16[512,512]{1,0:T(8,128)(2,1)S(1)} %reshape.60.placing, bf16[2,2048,512]{2,1,0:T(8,128)(2,1)S(1)} %copy-done.8), custom_call_target="tpu_custom_call" | custom-call | flops 4294967296 | bytes 8388608 | tf_op jit(solution)/shard_map/first/pallas_call | solution.py:147
  149.5 0.0 copy-start.5
  149.5 2.0 copy-done.5
  151.6 1.0 collective-permute-start
  152.5 1.2 add_convert_fusion.1
  153.7 0.4 collective-permute-start.7
  154.1 0.9 collective-permute-done.near
  154.9 1.2 add_convert_fusion.3
  156.1 0.4 collective-permute-start.1
  156.5 10.8 %collective-permute-done.7.far = bf16[512,512]{1,0:T(8,128)(2,1)S(1)} collective-permute-done((bf16[512,512]{1,0:T(8,128)(2,1)S(1)}, bf16[512,512]{1,0:T(8,128)(2,1)S(1)}, u32[]{:S(2)}, u32[]{:S(2)}) %collective-permute-start.7) | collective-permute-done | bytes 524320 | tf_op jit(solution)/shard_map/ppermute | solution.py:286
  167.3 1.3 collective-permute-start.8
  168.6 9.9 %collective-permute-done.1.far = bf16[512,512]{1,0:T(8,128)(2,1)S(1)} collective-permute-done((bf16[512,512]{1,0:T(8,128)(2,1)S(1)}, bf16[512,512]{1,0:T(8,128)(2,1)S(1)}, u32[]{:S(2)}, u32[]{:S(2)}) %collective-permute-start.1) | collective-permute-done | bytes 524320 | tf_op jit(solution)/shard_map/ppermute | solution.py:286
  178.5 0.9 collective-permute-start.2
  179.4 0.0 copy-start
  179.4 2.2 copy-done
  181.6 2.2 copy-done.3
  183.8 2.2 copy-done.9
  186.0 6.5 %middle.3 = (bf16[1024,2048]{1,0:T(8,128)(2,1)S(1)}, bf16[1024,512]{1,0:T(8,128)(2,1)S(1)}) custom-call(s32[1]{0:T(128)} %bitcast.place, bf16[1024,512]{1,0:T(8,128)(2,1)S(1)} %get-tuple-element.17.mine, bf16[1024,512]{1,0:T(8,128)(2,1)} %collective-permute-done.6.near, bf16[512,512]{1,0:T(8,128)(2,1)S(1)} %collective-permute-done.7.far, ...), custom_call_target="tpu_custom_call" | custom-call | flops 4294967296 | bytes 8388608 | tf_op jit(solution)/shard_map/middle/pallas_call | solution.py:202
  192.5 0.1 collective-permute-start.9
  192.6 6.5 %middle.2 = (bf16[1024,2048]{1,0:T(8,128)(2,1)S(1)}, bf16[1024,512]{1,0:T(8,128)(2,1)S(1)}) custom-call(s32[1]{0:T(128)} %bitcast.place, bf16[1024,512]{1,0:T(8,128)(2,1)S(1)} %get-tuple-element.13.mine, bf16[1024,512]{1,0:T(8,128)(2,1)} %collective-permute-done.near, bf16[512,512]{1,0:T(8,128)(2,1)S(1)} %collective-permute-done.1.far, ...), custom_call_target="tpu_custom_call" | custom-call | flops 4294967296 | bytes 8388608 | tf_op jit(solution)/shard_map/middle/pallas_call | solution.py:202
  199.1 0.6 collective-permute-start.3
  199.7 0.1 add_convert_fusion
  199.8 0.4 collective-permute-start.10
  200.2 1.8 collective-permute-done.3.near
  202.0 0.1 add_convert_fusion.2
  202.1 0.4 collective-permute-start.4
  202.5 10.9 %collective-permute-done.10.far = bf16[512,512]{1,0:T(8,128)(2,1)S(1)} collective-permute-done((bf16[512,512]{1,0:T(8,128)(2,1)S(1)}, bf16[512,512]{1,0:T(8,128)(2,1)S(1)}, u32[]{:S(2)}, u32[]{:S(2)}) %collective-permute-start.10) | collective-permute-done | bytes 524320 | tf_op jit(solution)/shard_map/ppermute | solution.py:286
  213.4 1.4 collective-permute-start.11
  214.7 9.8 %collective-permute-done.4.far = bf16[512,512]{1,0:T(8,128)(2,1)S(1)} collective-permute-done((bf16[512,512]{1,0:T(8,128)(2,1)S(1)}, bf16[512,512]{1,0:T(8,128)(2,1)S(1)}, u32[]{:S(2)}, u32[]{:S(2)}) %collective-permute-start.4) | collective-permute-done | bytes 524320 | tf_op jit(solution)/shard_map/ppermute | solution.py:286
  224.6 0.9 collective-permute-start.5
  225.5 0.0 collective-permute-done.11.across
  225.5 4.6 %last.2.rest_0_ = bf16[4,1,512,2048]{3,2,1,0:T(8,128)(2,1)} custom-call(s32[1]{0:T(128)} %bitcast.place, bf16[1024,512]{1,0:T(8,128)(2,1)S(1)} %get-tuple-element.19.mine, bf16[1024,512]{1,0:T(8,128)(2,1)S(1)} %collective-permute-done.9.near, bf16[512,512]{1,0:T(8,128)(2,1)S(1)} %collective-permute-done.10.far, ...), custom_call_target="tpu_custom_call" | custom-call | flops 2147483648 | bytes 12582912 | tf_op jit(solution)/shard_map/last/pallas_call | solution.py:260
  230.1 4.6 %last.3 = bf16[4,1,512,2048]{3,2,1,0:T(8,128)(2,1)} custom-call(s32[1]{0:T(128)} %bitcast.place, bf16[1024,512]{1,0:T(8,128)(2,1)S(1)} %get-tuple-element.15.mine, bf16[1024,512]{1,0:T(8,128)(2,1)S(1)} %collective-permute-done.3.near, bf16[512,512]{1,0:T(8,128)(2,1)S(1)} %collective-permute-done.4.far, ...), custom_call_target="tpu_custom_call", output_to_operand_aliasing={{}: (9, {})} | custom-call | flops 2147483648 | bytes 12582912 | tf_op jit(solution)/shard_map/last/pallas_call | solution.py:260
  (21 shorter events, 0.1 us)
Async XLA Ops:
  18.0 64.5 %all-to-all-start.1 = ((bf16[128,2,32,256]{3,2,1,0:T(8,128)(2,1)}), bf16[128,2,32,256]{3,2,1,0:T(8,128)(2,1)}, u32[]{:S(2)}, u32[]{:S(2)}) async-start(bf16[128,2,32,256]{3,2,1,0:T(8,128)(2,1)} %bitcast.9), calls=%async_computation.1 | async-start | bytes 8388608 | tf_op jit(solution)/shard_map/all_to_all | solution.py:314
  82.5 5.7 %copy-start.11 = (s32[64]{0:T(128)S(1)}, s32[64]{0:T(128)}, u32[]{:S(2)}) copy-start(s32[64]{0:T(128)} %param.7) | copy-start | bytes 772
  82.5 58.4 %all-to-all-start = ((bf16[128,2,32,256]{3,2,1,0:T(8,128)(2,1)}), bf16[128,2,32,256]{3,2,1,0:T(8,128)(2,1)}, u32[]{:S(2)}, u32[]{:S(2)}) async-start(bf16[128,2,32,256]{3,2,1,0:T(8,128)(2,1)} %bitcast.8), calls=%async_computation | async-start | bytes 8388608 | tf_op jit(solution)/shard_map/all_to_all | solution.py:314
  89.3 2.2 copy-start.7
  97.9 2.0 copy-start.2
  99.9 52.7 %collective-permute-start.6 = (bf16[1024,512]{1,0:T(8,128)(2,1)S(1)}, bf16[1024,512]{1,0:T(8,128)(2,1)}, u32[]{:S(2)}, u32[]{:S(2)}) collective-permute-start(bf16[1024,512]{1,0:T(8,128)(2,1)S(1)} %get-tuple-element.17.mine), channel_id=1, source_target_pairs={{0,1},{1,0},{2,3},{3,2},{4,5},{5,4},{6,7},{7,6},{8,9},{9,8},{10,11... | collective-permute-start | bytes 3145736 | tf_op jit(solution)/shard_map/ppermute | solution.py:281
  140.9 2.2 copy-start.8
  143.1 36.3 %copy-start.10 = (f32[2,2048]{1,0:T(2,128)S(1)}, f32[2,2048]{1,0:T(2,128)}, u32[]{:S(2)}) copy-start(f32[2,2048]{1,0:T(2,128)} %param.11) | copy-start | bytes 49156
  149.5 2.0 copy-start.5
  151.6 3.4 %collective-permute-start = (bf16[1024,512]{1,0:T(8,128)(2,1)S(1)}, bf16[1024,512]{1,0:T(8,128)(2,1)}, u32[]{:S(2)}, u32[]{:S(2)}) collective-permute-start(bf16[1024,512]{1,0:T(8,128)(2,1)S(1)} %get-tuple-element.13.mine), channel_id=1, source_target_pairs={{0,1},{1,0},{2,3},{3,2},{4,5},{5,4},{6,7},{7,6},{8,9},{9,8},{10,11... | collective-permute-start | bytes 3145736 | tf_op jit(solution)/shard_map/ppermute | solution.py:281
  153.7 13.6 %collective-permute-start.7 = (bf16[512,512]{1,0:T(8,128)(2,1)S(1)}, bf16[512,512]{1,0:T(8,128)(2,1)S(1)}, u32[]{:S(2)}, u32[]{:S(2)}) collective-permute-start(bf16[512,512]{1,0:T(8,128)(2,1)S(1)} %add_convert_fusion.1), channel_id=1, source_target_pairs={{0,2},{2,0},{1,3},{3,1},{4,6},{6,4},{5,7},{7,5},{8,10},{10,8},{9,1... | collective-permute-start | bytes 1572872 | tf_op jit(solution)/shard_map/ppermute | solution.py:286
  156.1 22.4 %collective-permute-start.1 = (bf16[512,512]{1,0:T(8,128)(2,1)S(1)}, bf16[512,512]{1,0:T(8,128)(2,1)S(1)}, u32[]{:S(2)}, u32[]{:S(2)}) collective-permute-start(bf16[512,512]{1,0:T(8,128)(2,1)S(1)} %add_convert_fusion.3), channel_id=1, source_target_pairs={{0,2},{2,0},{1,3},{3,1},{4,6},{6,4},{5,7},{7,5},{8,10},{10,8},{9,1... | collective-permute-start | bytes 1572872 | tf_op jit(solution)/shard_map/ppermute | solution.py:286
  167.3 12.1 %collective-permute-start.8 = (bf16[512,512]{1,0:T(8,128)(2,1)S(1)}, bf16[512,512]{1,0:T(8,128)(2,1)S(1)}, u32[]{:S(2)}, u32[]{:S(2)}) collective-permute-start(bf16[512,512]{1,0:T(8,128)(2,1)S(1)} %collective-permute-done.7.far), channel_id=1, source_target_pairs={{0,1},{1,0},{2,3},{3,2},{4,5},{5,4},{6,7},{7,6},{8,9},{9,8},{10,11... | collective-permute-start | bytes 1572872 | tf_op jit(solution)/shard_map/ppermute | solution.py:287
  178.5 14.1 %collective-permute-start.2 = (bf16[512,512]{1,0:T(8,128)(2,1)S(1)}, bf16[512,512]{1,0:T(8,128)(2,1)S(1)}, u32[]{:S(2)}, u32[]{:S(2)}) collective-permute-start(bf16[512,512]{1,0:T(8,128)(2,1)S(1)} %collective-permute-done.1.far), channel_id=1, source_target_pairs={{0,1},{1,0},{2,3},{3,2},{4,5},{5,4},{6,7},{7,6},{8,9},{9,8},{10,11... | collective-permute-start | bytes 1572872 | tf_op jit(solution)/shard_map/ppermute | solution.py:287
  179.4 2.2 copy-start
  181.6 2.2 copy-start.3
  183.8 2.2 copy-start.9
  186.0 6.6 %copy-start.1 = (bf16[2,512,2048]{2,1,0:T(8,128)(2,1)S(1)}, bf16[2,512,2048]{2,1,0:T(8,128)(2,1)}, u32[]{:S(2)}) copy-start(bf16[2,512,2048]{2,1,0:T(8,128)(2,1)} %up.7) | copy-start | bytes 12582916
  186.0 6.6 %copy-start.6 = (bf16[1024,2048]{1,0:T(8,128)(2,1)S(1)}, bf16[1024,2048]{1,0:T(8,128)(2,1)}, u32[]{:S(2)}) copy-start(bf16[1024,2048]{1,0:T(8,128)(2,1)} %copy-done.5) | copy-start | bytes 12582916
  192.5 7.2 %collective-permute-start.9 = (bf16[1024,512]{1,0:T(8,128)(2,1)S(1)}, bf16[1024,512]{1,0:T(8,128)(2,1)S(1)}, u32[]{:S(2)}, u32[]{:S(2)}) collective-permute-start(bf16[1024,512]{1,0:T(8,128)(2,1)S(1)} %get-tuple-element.19.mine), channel_id=1, source_target_pairs={{0,1},{1,0},{2,3},{3,2},{4,5},{5,4},{6,7},{7,6},{8,9},{9,8},{10,11... | collective-permute-start | bytes 3145736 | tf_op jit(solution)/shard_map/ppermute | solution.py:281
  192.6 32.9 %copy-start.4 = (bf16[1024,2048]{1,0:T(8,128)(2,1)S(1)}, bf16[1024,2048]{1,0:T(8,128)(2,1)}, u32[]{:S(2)}) copy-start(bf16[1024,2048]{1,0:T(8,128)(2,1)} %copy-done.2) | copy-start | bytes 12582916
  199.1 2.8 %collective-permute-start.3 = (bf16[1024,512]{1,0:T(8,128)(2,1)S(1)}, bf16[1024,512]{1,0:T(8,128)(2,1)S(1)}, u32[]{:S(2)}, u32[]{:S(2)}) collective-permute-start(bf16[1024,512]{1,0:T(8,128)(2,1)S(1)} %get-tuple-element.15.mine), channel_id=1, source_target_pairs={{0,1},{1,0},{2,3},{3,2},{4,5},{5,4},{6,7},{7,6},{8,9},{9,8},{10,11... | collective-permute-start | bytes 3145736 | tf_op jit(solution)/shard_map/ppermute | solution.py:281
  199.8 13.5 %collective-permute-start.10 = (bf16[512,512]{1,0:T(8,128)(2,1)S(1)}, bf16[512,512]{1,0:T(8,128)(2,1)S(1)}, u32[]{:S(2)}, u32[]{:S(2)}) collective-permute-start(bf16[512,512]{1,0:T(8,128)(2,1)S(1)} %add_convert_fusion), channel_id=1, source_target_pairs={{0,2},{2,0},{1,3},{3,1},{4,6},{6,4},{5,7},{7,5},{8,10},{10,8},{9,1... | collective-permute-start | bytes 1572872 | tf_op jit(solution)/shard_map/ppermute | solution.py:286
  202.1 22.5 %collective-permute-start.4 = (bf16[512,512]{1,0:T(8,128)(2,1)S(1)}, bf16[512,512]{1,0:T(8,128)(2,1)S(1)}, u32[]{:S(2)}, u32[]{:S(2)}) collective-permute-start(bf16[512,512]{1,0:T(8,128)(2,1)S(1)} %add_convert_fusion.2), channel_id=1, source_target_pairs={{0,2},{2,0},{1,3},{3,1},{4,6},{6,4},{5,7},{7,5},{8,10},{10,8},{9,1... | collective-permute-start | bytes 1572872 | tf_op jit(solution)/shard_map/ppermute | solution.py:286
  213.4 12.1 %collective-permute-start.11 = (bf16[512,512]{1,0:T(8,128)(2,1)S(1)}, bf16[512,512]{1,0:T(8,128)(2,1)S(1)}, u32[]{:S(2)}, u32[]{:S(2)}) collective-permute-start(bf16[512,512]{1,0:T(8,128)(2,1)S(1)} %collective-permute-done.10.far), channel_id=1, source_target_pairs={{0,1},{1,0},{2,3},{3,2},{4,5},{5,4},{6,7},{7,6},{8,9},{9,8},{10,11... | collective-permute-start | bytes 1572872 | tf_op jit(solution)/shard_map/ppermute | solution.py:287
  224.6 5.5 %collective-permute-start.5 = (bf16[512,512]{1,0:T(8,128)(2,1)S(1)}, bf16[512,512]{1,0:T(8,128)(2,1)S(1)}, u32[]{:S(2)}, u32[]{:S(2)}) collective-permute-start(bf16[512,512]{1,0:T(8,128)(2,1)S(1)} %collective-permute-done.4.far), channel_id=1, source_target_pairs={{0,1},{1,0},{2,3},{3,2},{4,5},{5,4},{6,7},{7,6},{8,9},{9,8},{10,11... | collective-permute-start | bytes 1572872 | tf_op jit(solution)/shard_map/ppermute | solution.py:287

commit v4 on v3

--- a/solution.py
+++ b/solution.py
@@ -25,11 +25,18 @@
 
 def lookup_kernel(layout, place, ids, tables, out, wide, evens, odds, staged, *rest):
     share, stride, offset, part, width, sources = layout
-    known, sems, moved = rest[:2], rest[2], rest[3]
+    known, sems, moved, narrow, loaded = rest[:2], rest[2], rest[3], rest[4], rest[5]
     slots, rows, _ = tables.shape
     step = pl.program_id(0)
     steps = pl.num_programs(0)
     run = width // 2 * part
+    tall = rows // 2
+
+    def load(piece):
+        slot, cut = piece // 2, pl.ds(piece % 2 * tall, tall)
+        return pltpu.make_async_copy(
+            tables.at[slot, cut, :], narrow.at[slot, cut, :], loaded.at[piece]
+        )
 
     def stage(destination):
         start = destination * stride + place[0] * share + offset
@@ -49,12 +56,16 @@
     def _():
         for destination in range(sources):
             stage(destination).start()
-        for slot in range(slots):
-            wide[pl.ds(slot * rows, rows), :] = tables[slot].astype(F32)
+        for piece in range(2 * slots):
+            load(piece).start()
         for destination in range(sources):
             stage(destination).wait()
         for which in range(2):
             fetch(0, which).start()
+        for piece in range(2 * slots):
+            load(piece).wait()
+            slot, first = piece // 2, piece % 2 * tall
+            wide[pl.ds(piece * tall, tall), :] = narrow[slot, pl.ds(first, tall), :].astype(F32)
 
     for which in range(2):
         fetch(step, which).wait()
@@ -82,7 +93,7 @@
 def looked_up(ids, tables, place, sources, groups, share, offset, part):
     slots, rows, emb = tables.shape
     count = sources * slots * part
-    width = 8
+    width = 4
     layout = (share, groups * share, offset, part, width, sources)
     return pl.pallas_call(
         functools.partial(lookup_kernel, layout),
@@ -91,7 +102,7 @@
             grid=(sources // width,),
             in_specs=[
                 pl.BlockSpec(memory_space=pltpu.HBM),
-                pl.BlockSpec((slots, rows, emb), lambda i, place: (0, 0, 0)),
+                pl.BlockSpec(memory_space=pltpu.HBM),
             ],
             out_specs=pl.BlockSpec(
                 (width, groups, slots, emb // groups, part), lambda i, place: (i, 0, 0, 0, 0)
@@ -105,6 +116,8 @@
                 pltpu.SMEM((slots, width // 2 * part), jnp.int32),
                 pltpu.SemaphoreType.DMA((sources,)),
                 pltpu.SemaphoreType.DMA((2,)),
+                pltpu.VMEM((slots, rows, emb), BF16),
+                pltpu.SemaphoreType.DMA((2 * slots,)),
             ],
         ),
         out_shape=jax.ShapeDtypeStruct((sources, groups, slots, emb // groups, part), BF16),

time: 235 us -> 234 us (level)
  transfers between devices with their start and end apart: 14 -> 14, of which waited for: 8 -> 8; matrix products, arithmetic and copies ran while one was open for 2% -> 2% of each run, Pallas kernels for 21% -> 20%
where the time goes in v4:
time: 234 us
  waiting for transfers between devices  119 us (51%)
  Pallas kernels  69.4 us (30%)
  starting transfers between devices  26.5 us (11%)
  local copies, waits for them, and re-layouts  15.5 us (7%)
  other arithmetic  3.08 us (1%)
    all_to_all x2, waiting for transfers between devices, per_device(): lax.all_to_all(looked.reshape(sources * groups, *shape[2:]), ('batch', 'm...  75.2 us
    ppermute x4, waiting for transfers between devices, summed(): far = lax.ppermute(pair, 'mp', CHIP)  41.4 us
    pallas_call x2, Pallas kernels, looked_up(): pl.pallas_call(functools.partial(lookup_kernel, layout), grid_spec=pltpu....  34.3 us
    all_to_all x2, starting transfers between devices, per_device(): lax.all_to_all(looked.reshape(sources * groups, *shape[2:]), ('batch', 'm...  17.6 us
    unnamed x24, local copies, waits for them, and re-layouts  14.9 us
    pallas_call x2, Pallas kernels, middle(): pl.pallas_call(middle_kernel, grid_spec=pltpu.PrefetchScalarGridSpec(num_...  13 us
    pallas_call x2, Pallas kernels, first(): pl.pallas_call(first_kernel, grid=(groups // many,), in_specs=[pl.BlockSp...  12.8 us
    pallas_call x2, Pallas kernels, last(): pl.pallas_call(last_kernel, grid_spec=pltpu.PrefetchScalarGridSpec(num_sc...  9.15 us
  transfers between devices with their start and end apart: 14, of which 8 were waited for; matrix products, arithmetic and copies ran while one was open for 2% of the time, Pallas kernels for 20%

profile of v4, /device:TPU:1, one launch (start us, length us, event | category | flops | bytes accessed | tf_op | source)
XLA Modules:
  0.0 233.9 jit_solution(13739761432741224163)
XLA Ops:
  0.0 17.2 %lookup.3 = bf16[32,4,2,32,256]{4,3,2,1,0:T(8,128)(2,1)} custom-call(s32[1]{0:T(128)} %bitcast.place, s32[2,65536]{1,0:T(2,128)} %ids.3, bf16[2,8192,128]{2,1,0:T(8,128)(2,1)} %tables.3), custom_call_target="tpu_custom_call" | custom-call | flops 16384000000 | bytes 4194304 | tf_op jit(solution)/shard_map/lookup/pallas_call | solution.py:98
  17.2 11.9 %all-to-all-start.1 = ((bf16[128,2,32,256]{3,2,1,0:T(8,128)(2,1)}), bf16[128,2,32,256]{3,2,1,0:T(8,128)(2,1)}, u32[]{:S(2)}, u32[]{:S(2)}) async-start(bf16[128,2,32,256]{3,2,1,0:T(8,128)(2,1)} %bitcast.9), calls=%async_computation.1 | async-start | bytes 8388608 | tf_op jit(solution)/shard_map/all_to_all | solution.py:327
  29.2 17.1 %lookup.2 = bf16[32,4,2,32,256]{4,3,2,1,0:T(8,128)(2,1)} custom-call(s32[1]{0:T(128)} %bitcast.place, s32[2,65536]{1,0:T(2,128)} %ids.3, bf16[2,8192,128]{2,1,0:T(8,128)(2,1)} %tables.3), custom_call_target="tpu_custom_call" | custom-call | flops 16384000000 | bytes 4194304 | tf_op jit(solution)/shard_map/lookup/pallas_call | solution.py:98
  46.3 35.4 %all-to-all-done.1 = bf16[128,2,32,256]{3,2,1,0:T(8,128)(2,1)} async-done(((bf16[128,2,32,256]{3,2,1,0:T(8,128)(2,1)}), bf16[128,2,32,256]{3,2,1,0:T(8,128)(2,1)}, u32[]{:S(2)}, u32[]{:S(2)}) %all-to-all-start.1) | async-done | bytes 4194336 | tf_op jit(solution)/shard_map/all_to_all | solution.py:327
  81.7 5.7 %all-to-all-start = ((bf16[128,2,32,256]{3,2,1,0:T(8,128)(2,1)}), bf16[128,2,32,256]{3,2,1,0:T(8,128)(2,1)}, u32[]{:S(2)}, u32[]{:S(2)}) async-start(bf16[128,2,32,256]{3,2,1,0:T(8,128)(2,1)} %bitcast.8), calls=%async_computation | async-start | bytes 8388608 | tf_op jit(solution)/shard_map/all_to_all | solution.py:327
  87.4 0.1 iota_compare_fusion
  87.5 0.4 and_convert_fusion
  87.9 0.6 reshape.60.placing
  88.5 0.0 copy-start.7
  88.5 2.2 copy-done.7
  90.7 6.4 %first.3 = (bf16[1024,2048]{1,0:T(8,128)(2,1)S(1)}, bf16[1024,512]{1,0:T(8,128)(2,1)S(1)}) custom-call(bf16[32,4,2,32,256]{4,3,2,1,0:T(8,128)(2,1)} %bitcast.4.moved, bf16[512,512]{1,0:T(8,128)(2,1)S(1)} %reshape.60.placing, bf16[2,2048,512]{2,1,0:T(8,128)(2,1)S(1)} %copy-done.7), custom_call_target="tpu_custom_call" | custom-call | flops 4294967296 | bytes 8388608 | tf_op jit(solution)/shard_map/first/pallas_call | solution.py:160
  97.1 2.0 copy-done.2
  99.1 1.3 collective-permute-start.6
  100.4 39.8 %all-to-all-done = bf16[128,2,32,256]{3,2,1,0:T(8,128)(2,1)} async-done(((bf16[128,2,32,256]{3,2,1,0:T(8,128)(2,1)}), bf16[128,2,32,256]{3,2,1,0:T(8,128)(2,1)}, u32[]{:S(2)}, u32[]{:S(2)}) %all-to-all-start) | async-done | bytes 4194336 | tf_op jit(solution)/shard_map/all_to_all | solution.py:327
  140.1 2.2 copy-done.8
  142.3 6.4 %first.2 = (bf16[1024,2048]{1,0:T(8,128)(2,1)S(1)}, bf16[1024,512]{1,0:T(8,128)(2,1)S(1)}) custom-call(bf16[32,4,2,32,256]{4,3,2,1,0:T(8,128)(2,1)} %bitcast.2.moved, bf16[512,512]{1,0:T(8,128)(2,1)S(1)} %reshape.60.placing, bf16[2,2048,512]{2,1,0:T(8,128)(2,1)S(1)} %copy-done.8), custom_call_target="tpu_custom_call" | custom-call | flops 4294967296 | bytes 8388608 | tf_op jit(solution)/shard_map/first/pallas_call | solution.py:160
  148.7 0.0 copy-start.5
  148.8 2.0 copy-done.5
  150.8 1.0 collective-permute-start
  151.7 0.0 collective-permute-done.6.near
  151.7 1.2 add_convert_fusion.1
  152.9 0.4 collective-permute-start.7
  153.3 0.9 collective-permute-done.near
  154.1 1.2 add_convert_fusion.3
  155.3 0.4 collective-permute-start.1
  155.7 10.8 %collective-permute-done.7.far = bf16[512,512]{1,0:T(8,128)(2,1)S(1)} collective-permute-done((bf16[512,512]{1,0:T(8,128)(2,1)S(1)}, bf16[512,512]{1,0:T(8,128)(2,1)S(1)}, u32[]{:S(2)}, u32[]{:S(2)}) %collective-permute-start.7) | collective-permute-done | bytes 524320 | tf_op jit(solution)/shard_map/ppermute | solution.py:299
  166.5 1.3 collective-permute-start.8
  167.8 9.9 %collective-permute-done.1.far = bf16[512,512]{1,0:T(8,128)(2,1)S(1)} collective-permute-done((bf16[512,512]{1,0:T(8,128)(2,1)S(1)}, bf16[512,512]{1,0:T(8,128)(2,1)S(1)}, u32[]{:S(2)}, u32[]{:S(2)}) %collective-permute-start.1) | collective-permute-done | bytes 524320 | tf_op jit(solution)/shard_map/ppermute | solution.py:299
  177.7 0.9 collective-permute-start.2
  178.6 0.0 copy-start
  178.6 2.2 copy-done
  180.8 2.2 copy-done.3
  183.0 2.2 copy-done.9
  185.2 6.5 %middle.3 = (bf16[1024,2048]{1,0:T(8,128)(2,1)S(1)}, bf16[1024,512]{1,0:T(8,128)(2,1)S(1)}) custom-call(s32[1]{0:T(128)} %bitcast.place, bf16[1024,512]{1,0:T(8,128)(2,1)S(1)} %get-tuple-element.17.mine, bf16[1024,512]{1,0:T(8,128)(2,1)} %collective-permute-done.6.near, bf16[512,512]{1,0:T(8,128)(2,1)S(1)} %collective-permute-done.7.far, ...), custom_call_target="tpu_custom_call" | custom-call | flops 4294967296 | bytes 8388608 | tf_op jit(solution)/shard_map/middle/pallas_call | solution.py:215
  191.7 0.1 collective-permute-start.9
  191.8 6.5 %middle.2 = (bf16[1024,2048]{1,0:T(8,128)(2,1)S(1)}, bf16[1024,512]{1,0:T(8,128)(2,1)S(1)}) custom-call(s32[1]{0:T(128)} %bitcast.place, bf16[1024,512]{1,0:T(8,128)(2,1)S(1)} %get-tuple-element.13.mine, bf16[1024,512]{1,0:T(8,128)(2,1)} %collective-permute-done.near, bf16[512,512]{1,0:T(8,128)(2,1)S(1)} %collective-permute-done.1.far, ...), custom_call_target="tpu_custom_call" | custom-call | flops 4294967296 | bytes 8388608 | tf_op jit(solution)/shard_map/middle/pallas_call | solution.py:215
  198.3 0.6 collective-permute-start.3
  198.9 0.1 add_convert_fusion
  199.0 0.4 collective-permute-start.10
  199.4 1.8 collective-permute-done.3.near
  201.2 0.1 add_convert_fusion.2
  201.3 0.4 collective-permute-start.4
  201.7 10.9 %collective-permute-done.10.far = bf16[512,512]{1,0:T(8,128)(2,1)S(1)} collective-permute-done((bf16[512,512]{1,0:T(8,128)(2,1)S(1)}, bf16[512,512]{1,0:T(8,128)(2,1)S(1)}, u32[]{:S(2)}, u32[]{:S(2)}) %collective-permute-start.10) | collective-permute-done | bytes 524320 | tf_op jit(solution)/shard_map/ppermute | solution.py:299
  212.6 1.4 collective-permute-start.11
  214.0 9.9 %collective-permute-done.4.far = bf16[512,512]{1,0:T(8,128)(2,1)S(1)} collective-permute-done((bf16[512,512]{1,0:T(8,128)(2,1)S(1)}, bf16[512,512]{1,0:T(8,128)(2,1)S(1)}, u32[]{:S(2)}, u32[]{:S(2)}) %collective-permute-start.4) | collective-permute-done | bytes 524320 | tf_op jit(solution)/shard_map/ppermute | solution.py:299
  223.8 0.9 collective-permute-start.5
  224.7 4.6 %last.2.rest_0_ = bf16[4,1,512,2048]{3,2,1,0:T(8,128)(2,1)} custom-call(s32[1]{0:T(128)} %bitcast.place, bf16[1024,512]{1,0:T(8,128)(2,1)S(1)} %get-tuple-element.19.mine, bf16[1024,512]{1,0:T(8,128)(2,1)S(1)} %collective-permute-done.9.near, bf16[512,512]{1,0:T(8,128)(2,1)S(1)} %collective-permute-done.10.far, ...), custom_call_target="tpu_custom_call" | custom-call | flops 2147483648 | bytes 12582912 | tf_op jit(solution)/shard_map/last/pallas_call | solution.py:273
  229.3 4.6 %last.3 = bf16[4,1,512,2048]{3,2,1,0:T(8,128)(2,1)} custom-call(s32[1]{0:T(128)} %bitcast.place, bf16[1024,512]{1,0:T(8,128)(2,1)S(1)} %get-tuple-element.15.mine, bf16[1024,512]{1,0:T(8,128)(2,1)S(1)} %collective-permute-done.3.near, bf16[512,512]{1,0:T(8,128)(2,1)S(1)} %collective-permute-done.4.far, ...), custom_call_target="tpu_custom_call", output_to_operand_aliasing={{}: (9, {})} | custom-call | flops 2147483648 | bytes 12582912 | tf_op jit(solution)/shard_map/last/pallas_call | solution.py:273
  (21 shorter events, 0.1 us)
Async XLA Ops:
  17.2 64.5 %all-to-all-start.1 = ((bf16[128,2,32,256]{3,2,1,0:T(8,128)(2,1)}), bf16[128,2,32,256]{3,2,1,0:T(8,128)(2,1)}, u32[]{:S(2)}, u32[]{:S(2)}) async-start(bf16[128,2,32,256]{3,2,1,0:T(8,128)(2,1)} %bitcast.9), calls=%async_computation.1 | async-start | bytes 8388608 | tf_op jit(solution)/shard_map/all_to_all | solution.py:327
  81.7 5.7 %copy-start.11 = (s32[64]{0:T(128)S(1)}, s32[64]{0:T(128)}, u32[]{:S(2)}) copy-start(s32[64]{0:T(128)} %param.7) | copy-start | bytes 772
  81.7 58.4 %all-to-all-start = ((bf16[128,2,32,256]{3,2,1,0:T(8,128)(2,1)}), bf16[128,2,32,256]{3,2,1,0:T(8,128)(2,1)}, u32[]{:S(2)}, u32[]{:S(2)}) async-start(bf16[128,2,32,256]{3,2,1,0:T(8,128)(2,1)} %bitcast.8), calls=%async_computation | async-start | bytes 8388608 | tf_op jit(solution)/shard_map/all_to_all | solution.py:327
  88.5 2.2 copy-start.7
  97.1 2.0 copy-start.2
  99.1 52.6 %collective-permute-start.6 = (bf16[1024,512]{1,0:T(8,128)(2,1)S(1)}, bf16[1024,512]{1,0:T(8,128)(2,1)}, u32[]{:S(2)}, u32[]{:S(2)}) collective-permute-start(bf16[1024,512]{1,0:T(8,128)(2,1)S(1)} %get-tuple-element.17.mine), channel_id=1, source_target_pairs={{0,1},{1,0},{2,3},{3,2},{4,5},{5,4},{6,7},{7,6},{8,9},{9,8},{10,11... | collective-permute-start | bytes 3145736 | tf_op jit(solution)/shard_map/ppermute | solution.py:294
  140.1 2.2 copy-start.8
  142.3 36.3 %copy-start.10 = (f32[2,2048]{1,0:T(2,128)S(1)}, f32[2,2048]{1,0:T(2,128)}, u32[]{:S(2)}) copy-start(f32[2,2048]{1,0:T(2,128)} %param.11) | copy-start | bytes 49156
  148.7 2.0 copy-start.5
  150.8 3.4 %collective-permute-start = (bf16[1024,512]{1,0:T(8,128)(2,1)S(1)}, bf16[1024,512]{1,0:T(8,128)(2,1)}, u32[]{:S(2)}, u32[]{:S(2)}) collective-permute-start(bf16[1024,512]{1,0:T(8,128)(2,1)S(1)} %get-tuple-element.13.mine), channel_id=1, source_target_pairs={{0,1},{1,0},{2,3},{3,2},{4,5},{5,4},{6,7},{7,6},{8,9},{9,8},{10,11... | collective-permute-start | bytes 3145736 | tf_op jit(solution)/shard_map/ppermute | solution.py:294
  152.9 13.6 %collective-permute-start.7 = (bf16[512,512]{1,0:T(8,128)(2,1)S(1)}, bf16[512,512]{1,0:T(8,128)(2,1)S(1)}, u32[]{:S(2)}, u32[]{:S(2)}) collective-permute-start(bf16[512,512]{1,0:T(8,128)(2,1)S(1)} %add_convert_fusion.1), channel_id=1, source_target_pairs={{0,2},{2,0},{1,3},{3,1},{4,6},{6,4},{5,7},{7,5},{8,10},{10,8},{9,1... | collective-permute-start | bytes 1572872 | tf_op jit(solution)/shard_map/ppermute | solution.py:299
  155.3 22.4 %collective-permute-start.1 = (bf16[512,512]{1,0:T(8,128)(2,1)S(1)}, bf16[512,512]{1,0:T(8,128)(2,1)S(1)}, u32[]{:S(2)}, u32[]{:S(2)}) collective-permute-start(bf16[512,512]{1,0:T(8,128)(2,1)S(1)} %add_convert_fusion.3), channel_id=1, source_target_pairs={{0,2},{2,0},{1,3},{3,1},{4,6},{6,4},{5,7},{7,5},{8,10},{10,8},{9,1... | collective-permute-start | bytes 1572872 | tf_op jit(solution)/shard_map/ppermute | solution.py:299
  166.5 12.1 %collective-permute-start.8 = (bf16[512,512]{1,0:T(8,128)(2,1)S(1)}, bf16[512,512]{1,0:T(8,128)(2,1)S(1)}, u32[]{:S(2)}, u32[]{:S(2)}) collective-permute-start(bf16[512,512]{1,0:T(8,128)(2,1)S(1)} %collective-permute-done.7.far), channel_id=1, source_target_pairs={{0,1},{1,0},{2,3},{3,2},{4,5},{5,4},{6,7},{7,6},{8,9},{9,8},{10,11... | collective-permute-start | bytes 1572872 | tf_op jit(solution)/shard_map/ppermute | solution.py:300
  177.7 14.1 %collective-permute-start.2 = (bf16[512,512]{1,0:T(8,128)(2,1)S(1)}, bf16[512,512]{1,0:T(8,128)(2,1)S(1)}, u32[]{:S(2)}, u32[]{:S(2)}) collective-permute-start(bf16[512,512]{1,0:T(8,128)(2,1)S(1)} %collective-permute-done.1.far), channel_id=1, source_target_pairs={{0,1},{1,0},{2,3},{3,2},{4,5},{5,4},{6,7},{7,6},{8,9},{9,8},{10,11... | collective-permute-start | bytes 1572872 | tf_op jit(solution)/shard_map/ppermute | solution.py:300
  178.6 2.2 copy-start
  180.8 2.2 copy-start.3
  183.0 2.2 copy-start.9
  185.2 6.6 %copy-start.1 = (bf16[2,512,2048]{2,1,0:T(8,128)(2,1)S(1)}, bf16[2,512,2048]{2,1,0:T(8,128)(2,1)}, u32[]{:S(2)}) copy-start(bf16[2,512,2048]{2,1,0:T(8,128)(2,1)} %up.7) | copy-start | bytes 12582916
  185.2 6.6 %copy-start.6 = (bf16[1024,2048]{1,0:T(8,128)(2,1)S(1)}, bf16[1024,2048]{1,0:T(8,128)(2,1)}, u32[]{:S(2)}) copy-start(bf16[1024,2048]{1,0:T(8,128)(2,1)} %copy-done.5) | copy-start | bytes 12582916
  191.7 7.2 %collective-permute-start.9 = (bf16[1024,512]{1,0:T(8,128)(2,1)S(1)}, bf16[1024,512]{1,0:T(8,128)(2,1)S(1)}, u32[]{:S(2)}, u32[]{:S(2)}) collective-permute-start(bf16[1024,512]{1,0:T(8,128)(2,1)S(1)} %get-tuple-element.19.mine), channel_id=1, source_target_pairs={{0,1},{1,0},{2,3},{3,2},{4,5},{5,4},{6,7},{7,6},{8,9},{9,8},{10,11... | collective-permute-start | bytes 3145736 | tf_op jit(solution)/shard_map/ppermute | solution.py:294
  191.8 32.9 %copy-start.4 = (bf16[1024,2048]{1,0:T(8,128)(2,1)S(1)}, bf16[1024,2048]{1,0:T(8,128)(2,1)}, u32[]{:S(2)}) copy-start(bf16[1024,2048]{1,0:T(8,128)(2,1)} %copy-done.2) | copy-start | bytes 12582916
  198.3 2.8 %collective-permute-start.3 = (bf16[1024,512]{1,0:T(8,128)(2,1)S(1)}, bf16[1024,512]{1,0:T(8,128)(2,1)S(1)}, u32[]{:S(2)}, u32[]{:S(2)}) collective-permute-start(bf16[1024,512]{1,0:T(8,128)(2,1)S(1)} %get-tuple-element.15.mine), channel_id=1, source_target_pairs={{0,1},{1,0},{2,3},{3,2},{4,5},{5,4},{6,7},{7,6},{8,9},{9,8},{10,11... | collective-permute-start | bytes 3145736 | tf_op jit(solution)/shard_map/ppermute | solution.py:294
  199.0 13.5 %collective-permute-start.10 = (bf16[512,512]{1,0:T(8,128)(2,1)S(1)}, bf16[512,512]{1,0:T(8,128)(2,1)S(1)}, u32[]{:S(2)}, u32[]{:S(2)}) collective-permute-start(bf16[512,512]{1,0:T(8,128)(2,1)S(1)} %add_convert_fusion), channel_id=1, source_target_pairs={{0,2},{2,0},{1,3},{3,1},{4,6},{6,4},{5,7},{7,5},{8,10},{10,8},{9,1... | collective-permute-start | bytes 1572872 | tf_op jit(solution)/shard_map/ppermute | solution.py:299
  201.3 22.5 %collective-permute-start.4 = (bf16[512,512]{1,0:T(8,128)(2,1)S(1)}, bf16[512,512]{1,0:T(8,128)(2,1)S(1)}, u32[]{:S(2)}, u32[]{:S(2)}) collective-permute-start(bf16[512,512]{1,0:T(8,128)(2,1)S(1)} %add_convert_fusion.2), channel_id=1, source_target_pairs={{0,2},{2,0},{1,3},{3,1},{4,6},{6,4},{5,7},{7,5},{8,10},{10,8},{9,1... | collective-permute-start | bytes 1572872 | tf_op jit(solution)/shard_map/ppermute | solution.py:299
  212.6 12.1 %collective-permute-start.11 = (bf16[512,512]{1,0:T(8,128)(2,1)S(1)}, bf16[512,512]{1,0:T(8,128)(2,1)S(1)}, u32[]{:S(2)}, u32[]{:S(2)}) collective-permute-start(bf16[512,512]{1,0:T(8,128)(2,1)S(1)} %collective-permute-done.10.far), channel_id=1, source_target_pairs={{0,1},{1,0},{2,3},{3,2},{4,5},{5,4},{6,7},{7,6},{8,9},{9,8},{10,11... | collective-permute-start | bytes 1572872 | tf_op jit(solution)/shard_map/ppermute | solution.py:300
  223.8 5.5 %collective-permute-start.5 = (bf16[512,512]{1,0:T(8,128)(2,1)S(1)}, bf16[512,512]{1,0:T(8,128)(2,1)S(1)}, u32[]{:S(2)}, u32[]{:S(2)}) collective-permute-start(bf16[512,512]{1,0:T(8,128)(2,1)S(1)} %collective-permute-done.4.far), channel_id=1, source_target_pairs={{0,1},{1,0},{2,3},{3,2},{4,5},{5,4},{6,7},{7,6},{8,9},{9,8},{10,11... | collective-permute-start | bytes 1572872 | tf_op jit(solution)/shard_map/ppermute | solution.py:300
